TPU v7x, 128 devices: a whole 4x4x4 slice. The times are simulated.
128 devices in a mesh: rows: 16 (over z, y), cols: 8 (over x, core).
Axes of the slice: x: 4, y: 4, z: 4, core: 2. Of those that a mesh axis runs over, the one named last changes fastest.
Arguments:
- train_query: bfloat16 [8192, 8192], P('rows', 'cols'), may hold values from -0.0625 to 0.0625
- low_query: bfloat16 [8192, 64], P('rows'), may hold values from -0.0625 to 0.0625
- high_query: bfloat16 [64, 8192], P(None, 'cols'), may hold values from -0.75 to 0.75
- train_key: bfloat16 [8192, 512], P('rows', 'cols'), may hold values from -0.0625 to 0.0625
- low_key: bfloat16 [8192, 64], P('rows'), may hold values from -0.0625 to 0.0625
- high_key: bfloat16 [64, 512], P(None, 'cols'), may hold values from -0.75 to 0.75
- train_value: bfloat16 [8192, 512], P('rows', 'cols'), may hold values from -0.0625 to 0.0625
- low_value: bfloat16 [8192, 64], P('rows'), may hold values from -0.0625 to 0.0625
- high_value: bfloat16 [64, 512], P(None, 'cols'), may hold values from -0.75 to 0.75
- norm_train: float32 [8192], P(('rows', 'cols')), may hold values from 0.25 to 1.75
- norm_step: float32 [8192], P(('rows', 'cols')), may hold values from -0.3 to 0.3
Outputs:
- serving_query: bfloat16 [8192, 8192], P('cols')
- serving_key: bfloat16 [512, 8192], P('cols')
- serving_value: bfloat16 [512, 8192], P('cols')
- serve_norm: bfloat16 [8192], replicated
All inputs are finite; a program needn't handle non-finite values.
Results may differ from a plain program's by a relative error of at most 0.001.
Values may be sent and summed in bfloat16 or wider, within the bound.
A program may use at most 128 MiB of HBM per device.

v0:
```python
import jax
import jax.numpy as jnp
from jax import lax
from jax.sharding import PartitionSpec as P

mix_rate = 1.0


def side_by_side(arrays, axis, dim, along):
    both = jnp.concatenate(arrays, axis=along)
    out, at, finished = (lax.all_gather(both, axis, axis=dim, tiled=True), 0, [])
    for a in arrays:
        finished.append(lax.slice_in_dim(out, at, at + a.shape[along], axis=along))
        at += a.shape[along]
    return tuple(finished)


def body(
    train_query,
    low_query,
    high_query,
    train_key,
    low_key,
    high_key,
    train_value,
    low_value,
    high_value,
    norm_train,
    norm_step,
):
    whole_query = train_query.astype(jnp.float32) + mix_rate * jnp.dot(
        low_query, high_query, preferred_element_type=jnp.float32
    )
    whole_key = train_key.astype(jnp.float32) + mix_rate * jnp.dot(
        low_key, high_key, preferred_element_type=jnp.float32
    )
    whole_value = train_value.astype(jnp.float32) + mix_rate * jnp.dot(
        low_value, high_value, preferred_element_type=jnp.float32
    )
    narrow_query, narrow_key, narrow_value = (
        whole_query.astype(jnp.bfloat16),
        whole_key.astype(jnp.bfloat16),
        whole_value.astype(jnp.bfloat16),
    )
    serving_query, serving_key, serving_value = side_by_side(
        (narrow_query, narrow_key, narrow_value), "rows", 0, 1
    )
    serving_query, serving_key, serving_value = (serving_query.T, serving_key.T, serving_value.T)
    serve_norm = lax.all_gather(
        (norm_train + norm_step).astype(jnp.bfloat16), ("rows", "cols"), axis=0, tiled=True
    )
    return (serving_query, serving_key, serving_value, serve_norm)


def solution(mesh):
    return jax.shard_map(
        body,
        mesh=mesh,
        in_specs=(
            P("rows", "cols"),
            P("rows", None),
            P(None, "cols"),
            P("rows", "cols"),
            P("rows", None),
            P(None, "cols"),
            P("rows", "cols"),
            P("rows", None),
            P(None, "cols"),
            P(("rows", "cols")),
            P(("rows", "cols")),
        ),
        out_specs=(P("cols", None), P("cols", None), P("cols", None), P()),
        check_vma=False,
    )
```

profile of v0, /device:TPU:1, one launch (start us, length us, event | category | flops | bytes accessed | tf_op | source)
XLA Modules:
  0.0 190.5 jit_solution(3674972838845907231)
XLA Ops:
  7.2 0.0 copy-start
  7.2 0.0 all-gather.2.cloned.1.call-start
  7.2 1.1 fusion
  8.3 0.1 copy.22
  8.5 1.1 fusion.1
  9.6 0.1 copy.23
  9.7 0.0 copy-done
  9.7 1.7 add_convert_fusion
  11.4 0.0 copy-start.1
  11.4 0.0 copy-start.2
  11.5 1.9 %concatenate.3 = bf16[512,1152]{1,0:T(8,128)(2,1)} concatenate(bf16[512,1024]{1,0:T(8,128)(2,1)S(1)} %add_convert_fusion, bf16[512,64]{1,0:T(8,128)(2,1)S(1)} %copy.22, bf16[512,64]{1,0:T(8,128)(2,1)S(1)} %copy.23), dimensions={1} | concatenate | bytes 2359296 | tf_op jit(solution)/shard_map/concatenate | solution.py:10
  13.4 0.0 all-gather.2.cloned.1.call-update
  13.4 0.0 copy-done.1
  13.4 0.0 copy-done.2
  13.5 0.2 dynamic-update-slice
  13.7 71.5 %all-reduce = bf16[8192]{0:T(1024)(128)(2,1)} all-reduce(bf16[8192]{0:T(1024)(128)(2,1)S(1)} %dynamic-update-slice), channel_id=1, replica_groups=mesh['rows'=16,'cols'=8] {'rows','cols'}, use_global_device_ids=true, to_apply=%add | all-reduce | flops 8192 | bytes 32768
  85.3 54.5 %all-gather.2.cloned.1.call-done = bf16[8192,1152]{1,0:T(8,128)(2,1)} async-done(((bf16[512,1152]{1,0:T(8,128)(2,1)}), bf16[8192,1152]{1,0:T(8,128)(2,1)}) %all-gather.2.cloned.1.call-update) | async-done | bytes 18874384 | tf_op jit(solution)/shard_map/all_gather | solution.py:11
  139.8 4.6 %slice_bitcast_fusion.1 = (bf16[64,8192]{0,1:T(8,128)(2,1)S(1)}, bf16[64,8192]{0,1:T(8,128)(2,1)}) fusion(bf16[8192,1152]{1,0:T(8,128)(2,1)} %all-gather.2.cloned.1.call-done), kind=kLoop, calls=%fused_computation.1 | loop fusion | bytes 4194304 | tf_op jit(solution)/shard_map/transpose | solution.py:48
  144.3 2.7 %copy.25 = bf16[64,8192]{1,0:T(8,128)(2,1)} copy(bf16[64,8192]{0,1:T(8,128)(2,1)} %get-tuple-element.13) | data formatting | bytes 2097152
  147.0 1.6 copy.26
  148.6 13.9 %slice_bitcast_fusion = bf16[1024,8192]{0,1:T(8,128)(2,1)} fusion(bf16[8192,1152]{1,0:T(8,128)(2,1)} %all-gather.2.cloned.1.call-done), kind=kLoop, calls=%fused_computation | loop fusion | bytes 33554432 | tf_op jit(solution)/shard_map/transpose | solution.py:48
  162.5 21.2 %copy.24 = bf16[1024,8192]{1,0:T(8,128)(2,1)} copy(bf16[1024,8192]{0,1:T(8,128)(2,1)} %slice_bitcast_fusion) | data formatting | bytes 33554432
  (2 shorter events, 0.0 us)
Async XLA Ops:
  7.2 2.5 %copy-start = (bf16[64,1024]{1,0:T(8,128)(2,1)S(1)}, bf16[64,1024]{1,0:T(8,128)(2,1)}, u32[]{:S(2)}) copy-start(bf16[64,1024]{1,0:T(8,128)(2,1)} %param.13) | copy-start | bytes 393220
  7.2 132.6 %all-gather.2.cloned.1.call-start = ((), (), s32[]{:S(2)}) async-start(), calls=%async_computation | async-start | bytes 20054016 | tf_op jit(solution)/shard_map/all_gather | solution.py:11
  11.4 2.0 %copy-start.1 = (f32[64]{0:T(128)S(1)}, f32[64]{0:T(128)}, u32[]{:S(2)}) copy-start(f32[64]{0:T(128)} %param.20) | copy-start | bytes 772
  11.4 2.0 %copy-start.2 = (f32[64]{0:T(128)S(1)}, f32[64]{0:T(128)}, u32[]{:S(2)}) copy-start(f32[64]{0:T(128)} %param.21) | copy-start | bytes 772
Sparse Core Ops, SparseCore 0:
  13.5 126.1 all-gather.1
where the time goes:
time: 191 us
  blocking collectives  71.5 us (37%)
  waiting for transfers between devices  54.5 us (29%)
  local copies, waits for them, and re-layouts  46.4 us (24%)
  between operations  14.1 us (7%)
  matrix products  3.93 us (2%)
    unnamed x1, blocking collectives  71.5 us
    all_gather x1, waiting for transfers between devices, side_by_side(): lax.all_gather(both, axis, axis=dim, tiled=True)  54.5 us
    unnamed x11, local copies, waits for them, and re-layouts  25.8 us
    transpose x2, local copies, waits for them, and re-layouts, body(): serving_query, serving_key, serving_value = (serving_query.T, serving_key...  18.4 us
  transfers between devices with their start and end apart: 1, of which 1 were waited for; matrix products, arithmetic and copies ran while one was open for 0% of the time, Pallas kernels for 0%

commit v1 on v0

v1 whole, which is shorter than its diff:
```python
import jax
import jax.numpy as jnp
from jax import lax
from jax.experimental import pallas as pl
from jax.experimental.pallas import tpu as pltpu
from jax.sharding import PartitionSpec as P

MESH = pl.DeviceIdType.MESH

SIDE = 4
QUARTERS = 4
LINKS = ((0, 1), (0, -1), (1, 0), (-1, 0))


def shift(off, d, sign=1):
    return ((off[0] + sign * d[0]) % SIDE, (off[1] + sign * d[1]) % SIDE)


def sends_of(link):
    d = LINKS[link]
    along_y = d[0] == 0
    first = (0, 1) if along_y else (2, 3)
    second = (2, 3) if along_y else (0, 1)
    positive = sum(d) > 0
    fwd_first = first[0] if positive else first[1]
    fwd_second = second[0] if positive else second[1]

    def across(n):
        return (n % SIDE, 0) if along_y else (0, n % SIDE)

    def behind(off):
        return shift(off, d, -1)

    own = (0, 0)
    return (
        (own, first[0]),
        (own, first[1]),
        (own, second[0]),
        (own, second[1]),
        (behind(own), fwd_first),
        (across(-1), second[0]),
        (across(1), second[0]),
        (across(-1), second[1]),
        (across(1), second[1]),
        (behind(own), fwd_second),
        (across(2), second[0]),
        (across(2), second[1]),
        (behind(across(-1)), fwd_second),
        (behind(across(1)), fwd_second),
        (behind(across(2)), fwd_second),
    )


SENDS = tuple(sends_of(link) for link in range(len(LINKS)))
SLOTS = len(SENDS[0])
ARRIVES = {
    (shift(off, LINKS[link], -1), quarter): (link, slot)
    for link in range(len(LINKS))
    for slot, (off, quarter) in enumerate(SENDS[link])
}
assert len(ARRIVES) == len(LINKS) * SLOTS == (SIDE * SIDE - 1) * QUARTERS
ORDER = (0, 2, 1, 3)


def gather_kernel(
    wide, tall,
    train_query, low_query, high_query,
    train_key, low_key, high_key,
    train_value, low_value, high_value,
    norm_train, norm_step,
    whole, norm,
    tq, lq, hq, tk, lk, hk, tv, lv, hv, nt, ns, near, ring,
    load_sem, send_sem, recv_sem, near_send, near_recv, ring_send, ring_recv,
):
    row, col = lax.axis_index("rows"), lax.axis_index("cols")
    z, y = row // SIDE, row % SIDE
    part = wide // QUARTERS
    width = tq.shape[1]

    def device(d):
        return (((z + d[0]) % SIDE) * SIDE + (y + d[1]) % SIDE, col)

    def at(off):
        return ((z + off[0]) % SIDE) * SIDE + (y + off[1]) % SIDE

    barrier = pltpu.get_barrier_semaphore()
    n_cols = near.shape[0]
    peers = [device(d) for d in LINKS] + [(row, (col + j) % n_cols) for j in range(1, n_cols)]
    for peer in peers:
        pl.semaphore_signal(barrier, inc=1, device_id=peer, device_id_type=MESH)

    loads = {}

    def load(name, src, dst):
        copy = pltpu.make_async_copy(src, dst, load_sem.at[len(loads)])
        copy.start()
        loads[name] = copy

    load("lq", low_query, lq)
    load("hq", high_query, hq)
    for q in ORDER:
        cols = pl.ds(q * part, part)
        load(q, train_query.at[:, cols], tq.at[:, cols])
        if q == ORDER[0]:
            load("tk", train_key, tk)
            load("lk", low_key, lk)
            load("hk", high_key, hk)
        if q == ORDER[1]:
            load("tv", train_value, tv)
            load("lv", low_value, lv)
            load("hv", high_value, hv)
    load("nt", norm_train, nt)
    load("ns", norm_step, ns)

    def merged(train, high, low):
        return train.astype(jnp.float32) + lax.dot_general(
            high, low, (((0,), (0,)), ((), ())), preferred_element_type=jnp.float32
        )

    def compute(q):
        cols = pl.ds(q * part, part)
        loads[q].wait()
        whole[row, q, 0:part, :] = merged(tq[:, cols].T, hq[:, cols], lq[...]).astype(whole.dtype)
        train, low, high = (tk, lk, hk) if q < 2 else (tv, lv, hv)
        small = merged(train[...], high[...], low[...]).astype(whole.dtype)
        half = small.shape[0] // 2
        whole[row, q, part:, :] = small[(q % 2) * half : (q % 2 + 1) * half, :]

    sent = []

    def send(link, slot):
        off, q = SENDS[link][slot]
        unit = whole.at[at(off), q]
        copy = pltpu.make_async_remote_copy(
            src_ref=unit,
            dst_ref=unit,
            send_sem=send_sem.at[link, slot],
            recv_sem=recv_sem.at[link, slot],
            device_id=device(LINKS[link]),
            device_id_type=MESH,
        )
        copy.start()
        sent.append(copy)

    arrived = set()

    def wait_unit(link, slot):
        if (link, slot) in arrived:
            return
        arrived.add((link, slot))
        off, q = SENDS[link][slot]
        unit = whole.at[at(shift(off, LINKS[link], -1)), q]
        pltpu.make_async_remote_copy(
            src_ref=unit,
            dst_ref=unit,
            send_sem=send_sem.at[link, slot],
            recv_sem=recv_sem.at[link, slot],
            device_id=device(LINKS[link]),
            device_id_type=MESH,
        ).wait_recv()

    loads["lq"].wait()
    loads["hq"].wait()
    for n, q in enumerate(ORDER):
        if n == 0:
            for name in ("tk", "lk", "hk"):
                loads[name].wait()
        if n == 1:
            for name in ("tv", "lv", "hv"):
                loads[name].wait()
        compute(q)
        if n == 0:
            pl.semaphore_wait(barrier, len(peers))
        for link in range(len(LINKS)):
            for slot in range(QUARTERS):
                if SENDS[link][slot][1] == q and slot < 2:
                    send(link, slot)
    for slot in (2, 3):
        for link in range(len(LINKS)):
            send(link, slot)

    loads["nt"].wait()
    loads["ns"].wait()
    fresh = nt[...] + ns[...]
    near[col] = jnp.concatenate([fresh, fresh], axis=1)

    def near_copy(j):
        return pltpu.make_async_remote_copy(
            src_ref=near.at[col],
            dst_ref=near.at[col],
            send_sem=near_send.at[j],
            recv_sem=near_recv.at[j],
            device_id=(row, (col + j) % n_cols),
            device_id_type=MESH,
        )

    def near_wait(j):
        slot = (col + n_cols - j) % n_cols
        pltpu.make_async_remote_copy(
            src_ref=near.at[slot],
            dst_ref=near.at[slot],
            send_sem=near_send.at[j],
            recv_sem=near_recv.at[j],
            device_id=(row, (col + j) % n_cols),
            device_id_type=MESH,
        ).wait_recv()

    near_copies = [near_copy(j) for j in range(1, n_cols)]
    for copy in near_copies:
        copy.start()

    def ring_copy(n, src, d):
        return pltpu.make_async_remote_copy(
            src_ref=src,
            dst_ref=src,
            send_sem=ring_send.at[n],
            recv_sem=ring_recv.at[n],
            device_id=device(d),
            device_id_type=MESH,
        )

    def column(dz):
        return ring.at[pl.ds(((z + dz) % SIDE) * SIDE, SIDE)]

    ring_copies = []

    def ring_start(n, src, d):
        copy = ring_copy(n, src, d)
        copy.start()
        ring_copies.append(copy)

    for slot in range(QUARTERS, SLOTS):
        for link in range(len(LINKS)):
            wait_unit(*ARRIVES[SENDS[link][slot]])
            send(link, slot)
        if slot == QUARTERS:
            for j in range(1, n_cols):
                near_wait(j)
            lane = lax.broadcasted_iota(jnp.int32, (1, near.shape[2]), 1)
            lines = [
                jnp.where(lane < near.shape[2] // 2, near[2 * k], near[2 * k + 1])
                for k in range(n_cols // 2)
            ]
            ring[row] = jnp.concatenate(lines, axis=0)
        if slot == QUARTERS + 1:
            ring_start(0, ring.at[row], (0, 1))
            ring_start(1, ring.at[row], (0, -1))
        if slot == QUARTERS + 2:
            ring_copy(0, ring.at[at((0, -1))], (0, 1)).wait_recv()
            ring_copy(1, ring.at[at((0, 1))], (0, -1)).wait_recv()
            ring_start(2, ring.at[at((0, -1))], (0, 1))
        if slot == QUARTERS + 3:
            ring_copy(2, ring.at[at((0, -2))], (0, 1)).wait_recv()
            ring_start(3, column(0), (1, 0))
            ring_start(4, column(0), (-1, 0))
        if slot == QUARTERS + 4:
            ring_copy(3, column(-1), (1, 0)).wait_recv()
            ring_copy(4, column(1), (-1, 0)).wait_recv()
            ring_start(5, column(-1), (1, 0))
        if slot == QUARTERS + 5:
            ring_copy(5, column(-2), (1, 0)).wait_recv()
            norm[...] = jnp.concatenate([ring[i] for i in range(SIDE * SIDE)], axis=0).astype(norm.dtype)

    for slot in range(SLOTS):
        for link in range(len(LINKS)):
            wait_unit(link, slot)
    for copy in sent + near_copies + ring_copies:
        copy.wait_send()


def write_kernel(whole, norm, out_query, out_key, out_value, out_norm, sem, norm_sem):
    blocks, quarters, rows, cols = whole.shape
    part = out_query.shape[0] // quarters
    last = pltpu.make_async_copy(norm, out_norm, norm_sem)
    last.start()

    def copies(r):
        at = pl.ds(pl.multiple_of(r * cols, cols), cols)
        half = rows - part
        for q in range(quarters):
            yield pltpu.make_async_copy(
                whole.at[r, q, pl.ds(0, part)], out_query.at[pl.ds(q * part, part), at], sem.at[r, q]
            )
        for q in range(quarters):
            target = out_key if q < 2 else out_value
            yield pltpu.make_async_copy(
                whole.at[r, q, pl.ds(part, half)], target.at[pl.ds((q % 2) * half, half), at], sem.at[r, quarters + q]
            )

    @pl.loop(0, blocks)
    def _(r):
        for copy in copies(r):
            copy.start()

    @pl.loop(0, blocks)
    def _(r):
        for copy in copies(r):
            copy.wait()

    last.wait()


def body(
    train_query, low_query, high_query,
    train_key, low_key, high_key,
    train_value, low_value, high_value,
    norm_train, norm_step,
):
    n_rows, n_cols = lax.axis_size("rows"), lax.axis_size("cols")
    depth, wide = train_query.shape
    tall = train_key.shape[1]
    rank = low_query.shape[1]
    unit = (wide + 2 * tall) // QUARTERS
    line = 2 * norm_train.shape[0]
    dtype = train_query.dtype
    anywhere = pl.BlockSpec(memory_space=pl.ANY)
    dma = pltpu.SemaphoreType.DMA

    def kernel(*refs):
        gather_kernel(wide, tall, *refs)

    whole, norm = pl.pallas_call(
        kernel,
        out_shape=(
            jax.ShapeDtypeStruct((n_rows, QUARTERS, unit, depth), dtype),
            jax.ShapeDtypeStruct((n_rows * n_cols // 2, line), dtype),
        ),
        in_specs=[anywhere] * 11,
        out_specs=(pl.BlockSpec(memory_space=pltpu.VMEM), pl.BlockSpec(memory_space=pltpu.VMEM)),
        scratch_shapes=[
            pltpu.VMEM((depth, wide), dtype),
            pltpu.VMEM((rank, depth), dtype),
            pltpu.VMEM((rank, wide), dtype),
            pltpu.VMEM((tall, depth), dtype),
            pltpu.VMEM((rank, depth), dtype),
            pltpu.VMEM((rank, tall), dtype),
            pltpu.VMEM((tall, depth), dtype),
            pltpu.VMEM((rank, depth), dtype),
            pltpu.VMEM((rank, tall), dtype),
            pltpu.VMEM((1, line // 2), jnp.float32),
            pltpu.VMEM((1, line // 2), jnp.float32),
            pltpu.VMEM((n_cols, 1, line), jnp.float32),
            pltpu.VMEM((n_rows, n_cols // 2, line), jnp.float32),
            dma((15,)),
            dma((len(LINKS), SLOTS)),
            dma((len(LINKS), SLOTS)),
            dma((n_cols,)),
            dma((n_cols,)),
            dma((6,)),
            dma((6,)),
        ],
        compiler_params=pltpu.CompilerParams(
            collective_id=0, has_side_effects=True, vmem_limit_bytes=32 * 2**20
        ),
        name="gather",
    )(
        *(
            pltpu.with_memory_space_constraint(x, pltpu.HBM)
            for x in (
                train_query, low_query.T, high_query,
                train_key.T, low_key.T, high_key,
                train_value.T, low_value.T, high_value,
                norm_train.reshape(1, -1), norm_step.reshape(1, -1),
            )
        )
    )
    out_query, out_key, out_value, out_norm = pl.pallas_call(
        write_kernel,
        out_shape=(
            jax.ShapeDtypeStruct((wide, n_rows * depth), dtype),
            jax.ShapeDtypeStruct((tall, n_rows * depth), dtype),
            jax.ShapeDtypeStruct((tall, n_rows * depth), dtype),
            jax.ShapeDtypeStruct(norm.shape, dtype),
        ),
        in_specs=[anywhere] * 2,
        out_specs=[anywhere] * 4,
        scratch_shapes=[dma((n_rows, 2 * QUARTERS)), dma(())],
        compiler_params=pltpu.CompilerParams(vmem_limit_bytes=4 * 2**20),
        name="write",
    )(whole, norm)
    return out_query, out_key, out_value, out_norm.reshape(-1)


def solution(mesh):
    return jax.shard_map(
        body,
        mesh=mesh,
        in_specs=(
            P("rows", "cols"),
            P("rows", None),
            P(None, "cols"),
            P("rows", "cols"),
            P("rows", None),
            P(None, "cols"),
            P("rows", "cols"),
            P("rows", None),
            P(None, "cols"),
            P(("rows", "cols")),
            P(("rows", "cols")),
        ),
        out_specs=(P("cols", None), P("cols", None), P("cols", None), P()),
        check_vma=False,
    )
```

time: 191 us -> 114 us (0.60)
  Pallas kernels: 0 us -> 113 us
  blocking collectives: 71.5 us -> 0 us
  waiting for transfers between devices: 54.5 us -> 0 us
  local copies, waits for them, and re-layouts: 46.4 us -> 0 us
  between operations: 14.1 us -> 0.64 us
  matrix products: 3.93 us -> 0 us
    pallas_call x0 -> x2, Pallas kernels: none -> 113 us  [the longest x1 106 us: body(): pl.pallas_call(kernel, out_shape=(jax.ShapeDtypeStruct((n_rows, QUARTERS,...]
    unnamed x1 -> x0, blocking collectives: 71.5 us -> none
    all_gather x1 -> x0, waiting for transfers between devices: 54.5 us -> none  [side_by_side(): lax.all_gather(both, axis, axis=dim, tiled=True)]
    unnamed x11 -> x0, local copies, waits for them, and re-layouts: 25.8 us -> none
    transpose x2 -> x0, local copies, waits for them, and re-layouts: 18.4 us -> none  [body(): serving_query, serving_key, serving_value = (serving_query.T, serving_key...]
    dot_general x3 -> x0, matrix products: 3.93 us -> none  [the longest x1 1.72 us: body(): jnp.dot(low_query, high_query, preferred_element_type=jnp.float32)]
    concatenate x1 -> x0, local copies, waits for them, and re-layouts: 1.93 us -> none  [side_by_side(): both = jnp.concatenate(arrays, axis=along)]
  transfers between devices with their start and end apart: 1 -> 0, of which waited for: 1 -> 0; matrix products, arithmetic and copies ran while one was open for 0% -> 0% of each run, Pallas kernels for 0% -> 0%
where the time goes in v1:
time: 114 us
  Pallas kernels  113 us (99%)
    pallas_call x1, Pallas kernels, body(): pl.pallas_call(kernel, out_shape=(jax.ShapeDtypeStruct((n_rows, QUARTERS,...  106 us
    pallas_call x1, Pallas kernels, body(): pl.pallas_call(write_kernel, out_shape=(jax.ShapeDtypeStruct((wide, n_row...  7.52 us

profile of v1, /device:TPU:1, one launch (start us, length us, event | category | flops | bytes accessed | tf_op | source)
XLA Modules:
  0.0 113.8 jit_solution(570801912475205070)
XLA Ops:
  0.6 105.6 %gather.1 = (bf16[16,4,288,512]{3,2,1,0:T(8,128)(2,1)S(1)}, bf16[64,128]{1,0:T(8,128)(2,1)S(1)}) custom-call(bf16[512,1024]{1,0:T(8,128)(2,1)} %refs_0_.1, bf16[64,512]{1,0:T(8,128)(2,1)} %bitcast.8, bf16[64,1024]{1,0:T(8,128)(2,1)} %refs_2_.1, bf16[64,512]{1,0:T(8,128)(2,1)} %bitcast.9, bf16[64,512]{1,0:T(8,128)(2,1)} %bitcast.10, bf16[64,64]{1,0:T(8,128)(2,1)} %refs_5_.1, ...), custom_call_target="tpu_custom_call" | custom-call | tf_op jit(solution)/shard_map/gather/pallas_call | solution.py:322
  106.3 7.5 %write.1 = (bf16[1024,8192]{1,0:T(8,128)(2,1)}, bf16[64,8192]{1,0:T(8,128)(2,1)}, bf16[64,8192]{1,0:T(8,128)(2,1)}, bf16[64,128]{1,0:T(8,128)(2,1)}) custom-call(bf16[16,4,288,512]{3,2,1,0:T(8,128)(2,1)S(1)} %get-tuple-element.10.whole, bf16[64,128]{1,0:T(8,128)(2,1)S(1)} %get-tuple-element.11.norm), custom_call_target="tpu_custom_call" | custom-call | tf_op jit(solution)/shard_map/write/pallas_call | solution.py:367

commit v2 on v0

v2 whole, which is shorter than its diff:
```python
import jax
import jax.numpy as jnp
from jax import lax
from jax.experimental import pallas as pl
from jax.experimental.pallas import tpu as pltpu
from jax.sharding import PartitionSpec as P

MESH = pl.DeviceIdType.MESH

SIDE = 4
QUARTERS = 4
CORES = 2
LINKS = ((0, 1), (0, -1), (1, 0), (-1, 0))
ORDER = (0, 2, 1, 3)
LATE = 1
SPLIT = 12


def shift(off, d, sign=1):
    return ((off[0] + sign * d[0]) % SIDE, (off[1] + sign * d[1]) % SIDE)


def sends_of(link):
    d = LINKS[link]
    along_y = d[0] == 0
    first = (0, 1) if along_y else (2, 3)
    second = (2, 3) if along_y else (0, 1)
    positive = sum(d) > 0
    fwd_first = first[0] if positive else first[1]
    fwd_second = second[0] if positive else second[1]

    def across(n):
        return (n % SIDE, 0) if along_y else (0, n % SIDE)

    def behind(off):
        return shift(off, d, -1)

    own = (0, 0)
    return tuple((own, q) for q in ORDER) + (
        (behind(own), fwd_first),
        (across(-1), second[0]),
        (across(1), second[0]),
        (across(-1), second[1]),
        (across(1), second[1]),
        (behind(own), fwd_second),
        (across(2), second[0]),
        (across(2), second[1]),
        (behind(across(-1)), fwd_second),
        (behind(across(1)), fwd_second),
        (behind(across(2)), fwd_second),
    )


SENDS = tuple(sends_of(link) for link in range(len(LINKS)))
SLOTS = len(SENDS[0])
UNITS = [(link, slot) for slot in range(SLOTS) for link in range(len(LINKS))]


def arriving(link, slot):
    off, quarter = SENDS[link][slot]
    return shift(off, LINKS[link], -1), quarter


ARRIVES = {arriving(*unit): unit for unit in UNITS}
assert len(ARRIVES) == len(UNITS) == (SIDE * SIDE - 1) * QUARTERS
LAST = [unit for unit in UNITS if unit[1] >= SPLIT]
assert all(ARRIVES[SENDS[link][slot]][1] < SPLIT for link, slot in LAST)


class Place:
    def __init__(self):
        self.row, self.col = lax.axis_index("rows"), lax.axis_index("cols")
        self.z, self.y = self.row // SIDE, self.row % SIDE
        self.x, self.core = self.col // CORES, self.col % CORES

    def at(self, off):
        return ((self.z + off[0]) % SIDE) * SIDE + (self.y + off[1]) % SIDE

    def neighbour(self, d):
        return (self.at(d), self.col)

    def partner(self):
        return (self.row, self.x * CORES + 1 - self.core)

    def along_x(self, n):
        return (self.row, ((self.x + n) % SIDE) * CORES + self.core)


def remote(src, dst, send_sem, recv_sem, device):
    return pltpu.make_async_remote_copy(
        src_ref=src, dst_ref=dst, send_sem=send_sem, recv_sem=recv_sem, device_id=device, device_id_type=MESH
    )


def signal_all(barrier, devices):
    for device in devices:
        pl.semaphore_signal(barrier, inc=1, device_id=device, device_id_type=MESH)


def gather_kernel(
    train_query, low_query, high_query,
    train_key, low_key, high_key,
    train_value, low_value, high_value,
    norm_train, norm_step,
    whole, lines,
    tq, lq, hq, tk, lk, hk, tv, lv, hv, nt, ns, pair, ring,
    load_sem, send_sem, recv_sem, pair_sem, ring_send, ring_recv,
):
    me = Place()
    wide = tq.shape[1]
    part = wide // QUARTERS

    barrier = pltpu.get_barrier_semaphore()
    peers = [me.neighbour(d) for d in LINKS] + [me.partner()]
    signal_all(barrier, peers)

    loads = {}

    def load(name, src, dst):
        copy = pltpu.make_async_copy(src, dst, load_sem.at[len(loads)])
        copy.start()
        loads[name] = copy

    load("lq", low_query, lq)
    load("hq", high_query, hq)
    for n, q in enumerate(ORDER):
        cols = pl.ds(q * part, part)
        load(q, train_query.at[:, cols], tq.at[:, cols])
        if n == 0:
            load("tk", train_key, tk)
            load("lk", low_key, lk)
            load("hk", high_key, hk)
        if n == 1:
            load("tv", train_value, tv)
            load("lv", low_value, lv)
            load("hv", high_value, hv)
    load("nt", norm_train, nt)
    load("ns", norm_step, ns)

    def merged(train, high, low):
        return train.astype(jnp.float32) + lax.dot_general(
            high, low, (((0,), (0,)), ((), ())), preferred_element_type=jnp.float32
        )

    def compute(q):
        cols = pl.ds(q * part, part)
        loads[q].wait()
        whole[me.row, q, 0:part, :] = merged(tq[:, cols].T, hq[:, cols], lq[...]).astype(whole.dtype)
        train, low, high = (tk, lk, hk) if q < 2 else (tv, lv, hv)
        small = merged(train[...], high[...], low[...]).astype(whole.dtype)
        half = small.shape[0] // 2
        whole[me.row, q, part:, :] = small[(q % 2) * half : (q % 2 + 1) * half, :]

    def unit_copy(link, slot, what):
        off, q = what
        unit = whole.at[me.at(off), q]
        return remote(unit, unit, send_sem.at[link, slot], recv_sem.at[link, slot], me.neighbour(LINKS[link]))

    def send(link, slot):
        unit_copy(link, slot, SENDS[link][slot]).start()

    def arrive(link, slot):
        unit_copy(link, slot, arriving(link, slot)).wait_recv()

    loads["lq"].wait()
    loads["hq"].wait()
    for n, q in enumerate(ORDER):
        if n == 0:
            for name in ("tk", "lk", "hk"):
                loads[name].wait()
        if n == 1:
            for name in ("tv", "lv", "hv"):
                loads[name].wait()
        compute(q)
        if n == 0:
            pl.semaphore_wait(barrier, len(peers))
        for link in range(len(LINKS)):
            send(link, n)

    loads["nt"].wait()
    loads["ns"].wait()
    fresh = nt[...] + ns[...]
    pair[me.core] = jnp.concatenate([fresh, fresh], axis=1)

    def pair_copy(slot):
        return remote(pair.at[slot], pair.at[slot], pair_sem.at[0], pair_sem.at[1], me.partner())

    pair_copy(me.core).start()

    def ring_copy(n, src, d):
        return remote(src, src, ring_send.at[n], ring_recv.at[n], me.neighbour(d))

    def column(dz):
        return ring.at[pl.ds(((me.z + dz) % SIDE) * SIDE, SIDE)]

    ring_copies = []

    def ring_start(n, src, d):
        copy = ring_copy(n, src, d)
        copy.start()
        ring_copies.append(copy)

    def norm_step_of(slot):
        step = slot - QUARTERS
        if step == 0:
            pair_copy(1 - me.core).wait_recv()
            lane = lax.broadcasted_iota(jnp.int32, (1, pair.shape[2]), 1)
            ring[me.row] = jnp.where(lane < pair.shape[2] // CORES, pair[0], pair[1])
        if step == 1:
            ring_start(0, ring.at[me.row], (0, 1))
            ring_start(1, ring.at[me.row], (0, -1))
        if step == 2:
            ring_copy(0, ring.at[me.at((0, -1))], (0, 1)).wait_recv()
            ring_copy(1, ring.at[me.at((0, 1))], (0, -1)).wait_recv()
            ring_start(2, ring.at[me.at((0, -1))], (0, 1))
        if step == 3:
            ring_copy(2, ring.at[me.at((0, -2))], (0, 1)).wait_recv()
            ring_start(3, column(0), (1, 0))
            ring_start(4, column(0), (-1, 0))
        if step == 4:
            ring_copy(3, column(-1), (1, 0)).wait_recv()
            ring_copy(4, column(1), (-1, 0)).wait_recv()
            ring_start(5, column(-1), (1, 0))
        if step == 5:
            ring_copy(5, column(-2), (1, 0)).wait_recv()
            lines[...] = jnp.concatenate([ring[i] for i in range(SIDE * SIDE)], axis=0)

    arrived = set()

    def arrive_once(unit):
        if unit not in arrived:
            arrived.add(unit)
            arrive(*unit)

    for slot in range(QUARTERS, SPLIT):
        for link in range(len(LINKS)):
            arrive_once(ARRIVES[SENDS[link][slot]])
            send(link, slot)
        norm_step_of(slot)
    for unit in LAST:
        arrive_once(ARRIVES[SENDS[unit[0]][unit[1]]])

    @pl.when(me.core != LATE)
    def _():
        for unit in LAST:
            send(*unit)

    for unit in UNITS:
        if unit not in LAST:
            arrive_once(unit)

    @pl.when(me.core != LATE)
    def _():
        for unit in LAST:
            arrive(*unit)
        for unit in LAST:
            unit_copy(*unit, SENDS[unit[0]][unit[1]]).wait_send()

    for unit in UNITS:
        if unit not in LAST:
            unit_copy(*unit, SENDS[unit[0]][unit[1]]).wait_send()
    pair_copy(me.core).wait_send()
    for copy in ring_copies:
        copy.wait_send()


def finish_kernel(
    whole, lines, token,
    rest, norm,
    all_lines, ordered, send_sem, recv_sem, line_send, line_recv, norm_sem,
):
    del token
    me = Place()
    barrier = pltpu.get_barrier_semaphore()
    norm_copy = remote(norm, norm, norm_sem.at[0], norm_sem.at[1], me.partner())

    @pl.when(me.core == LATE)
    def _():
        signal_all(barrier, [me.neighbour(d) for d in LINKS] + [me.partner()])
        pl.semaphore_wait(barrier, len(LINKS))
        copies = []
        for link, slot in LAST:
            off, q = SENDS[link][slot]
            n = slot - SPLIT
            copy = remote(
                whole.at[me.at(off), q],
                rest.at[link, n],
                send_sem.at[link, n],
                recv_sem.at[link, n],
                me.neighbour(LINKS[link]),
            )
            copy.start()
            copies.append(copy)
        norm_copy.wait_recv()
        for copy in copies:
            copy.wait()

    @pl.when(me.core != LATE)
    def _():
        steps = range(1, SIDE)
        signal_all(barrier, [me.along_x(n) for n in steps])
        pl.semaphore_wait(barrier, len(steps) + 1)

        def line_copy(n, x):
            return remote(lines, all_lines.at[x], line_send.at[n - 1], line_recv.at[n - 1], me.along_x(n))

        for n in steps:
            line_copy(n, me.x).start()
        all_lines[me.x] = lines[...]
        for n in steps:
            line_copy(n, (me.x - n) % SIDE).wait_recv()
        for x in range(SIDE):
            ordered[pl.Slice(x, SIDE * SIDE, SIDE), :] = all_lines[x]
        norm[...] = ordered[...].astype(norm.dtype)
        norm_copy.start()
        for n in steps:
            line_copy(n, me.x).wait_send()
        norm_copy.wait_send()


def out_copies(source, block, quarter, outs, sem):
    out_query, out_key, out_value = outs
    rows, depth = source.shape
    part = out_query.shape[0] // QUARTERS
    half = rows - part
    at = pl.ds(pl.multiple_of(block * depth, depth), depth)
    small = (out_key if quarter < 2 else out_value).at[pl.ds((quarter % 2) * half, half), at]
    return (
        pltpu.make_async_copy(source.at[pl.ds(0, part)], out_query.at[pl.ds(quarter * part, part), at], sem.at[0]),
        pltpu.make_async_copy(source.at[pl.ds(part, half)], small, sem.at[1]),
    )


def run_copies(copies):
    for copy in copies:
        copy.start()
    for copy in copies:
        copy.wait()


BLOCKS = [(dz, dy) for dz in range(SIDE) for dy in range(SIDE)]
PIECES = [(off, q) for off in BLOCKS for q in range(QUARTERS)]


def write_kernel(whole, out_query, out_key, out_value, token, sem):
    me = Place()
    outs = (out_query, out_key, out_value)
    token[...] = jnp.zeros_like(token)
    late = {arriving(*unit) for unit in LAST}

    @pl.when(me.core == LATE)
    def _():
        copies = []
        for n, (off, q) in enumerate(PIECES):
            if (off, q) not in late:
                block = me.at(off)
                copies.extend(out_copies(whole.at[block, q], block, q, outs, sem.at[n]))
        run_copies(copies)


def write_rest_kernel(
    whole, rest, norm, in_query, in_key, in_value, out_query, out_key, out_value, out_norm, sem, norm_sem
):
    del in_query, in_key, in_value
    me = Place()
    outs = (out_query, out_key, out_value)
    norm_copy = pltpu.make_async_copy(norm, out_norm, norm_sem)
    norm_copy.start()

    @pl.when(me.core == LATE)
    def _():
        copies = []
        for n, (link, slot) in enumerate(LAST):
            off, q = arriving(link, slot)
            copies.extend(out_copies(rest.at[link, slot - SPLIT], me.at(off), q, outs, sem.at[n]))
        run_copies(copies)

    @pl.when(me.core != LATE)
    def _():
        copies = []
        for n, (off, q) in enumerate(PIECES):
            block = me.at(off)
            copies.extend(out_copies(whole.at[block, q], block, q, outs, sem.at[n]))
        run_copies(copies)

    norm_copy.wait()


def body(
    train_query, low_query, high_query,
    train_key, low_key, high_key,
    train_value, low_value, high_value,
    norm_train, norm_step,
):
    n_rows, n_cols = lax.axis_size("rows"), lax.axis_size("cols")
    depth, wide = train_query.shape
    tall = train_key.shape[1]
    rank = low_query.shape[1]
    unit = (wide + 2 * tall) // QUARTERS
    values = norm_train.shape[0]
    line = CORES * values
    dtype = train_query.dtype
    f32 = jnp.float32
    anywhere = pl.BlockSpec(memory_space=pl.ANY)
    vmem = pl.BlockSpec(memory_space=pltpu.VMEM)
    dma = pltpu.SemaphoreType.DMA
    shape = jax.ShapeDtypeStruct
    outs = [shape((wide, n_rows * depth), dtype)] + [shape((tall, n_rows * depth), dtype)] * 2

    def pin(space, *arrays):
        return [pltpu.with_memory_space_constraint(a, space) for a in arrays]

    whole, lines = pl.pallas_call(
        gather_kernel,
        out_shape=(shape((n_rows, QUARTERS, unit, depth), dtype), shape((n_rows, line), f32)),
        in_specs=[anywhere] * 11,
        out_specs=(vmem, vmem),
        scratch_shapes=[
            pltpu.VMEM((depth, wide), dtype),
            pltpu.VMEM((rank, depth), dtype),
            pltpu.VMEM((rank, wide), dtype),
            pltpu.VMEM((tall, depth), dtype),
            pltpu.VMEM((rank, depth), dtype),
            pltpu.VMEM((rank, tall), dtype),
            pltpu.VMEM((tall, depth), dtype),
            pltpu.VMEM((rank, depth), dtype),
            pltpu.VMEM((rank, tall), dtype),
            pltpu.VMEM((1, values), f32),
            pltpu.VMEM((1, values), f32),
            pltpu.VMEM((CORES, 1, line), f32),
            pltpu.VMEM((n_rows, 1, line), f32),
            dma((14,)),
            dma((len(LINKS), SLOTS)),
            dma((len(LINKS), SLOTS)),
            dma((2,)),
            dma((6,)),
            dma((6,)),
        ],
        compiler_params=pltpu.CompilerParams(
            collective_id=0, has_side_effects=True, vmem_limit_bytes=24 * 2**20
        ),
        name="gather",
    )(
        *pin(
            pltpu.HBM,
            train_query, low_query.T, high_query,
            train_key.T, low_key.T, high_key,
            train_value.T, low_value.T, high_value,
            norm_train.reshape(1, -1), norm_step.reshape(1, -1),
        )
    )
    out_query, out_key, out_value, token = pl.pallas_call(
        write_kernel,
        out_shape=(*outs, shape((8, 128), f32)),
        in_specs=[vmem],
        out_specs=[anywhere] * 3 + [vmem],
        scratch_shapes=[dma((len(PIECES), 2))],
        compiler_params=pltpu.CompilerParams(vmem_limit_bytes=4 * 2**20),
        name="write",
    )(*pin(pltpu.VMEM, whole))
    rest, norm = pl.pallas_call(
        finish_kernel,
        out_shape=(
            shape((len(LINKS), SLOTS - SPLIT, unit, depth), dtype),
            shape((n_rows * n_cols // CORES, line), dtype),
        ),
        in_specs=[vmem] * 3,
        out_specs=(vmem, vmem),
        scratch_shapes=[
            pltpu.VMEM((SIDE, n_rows, line), f32),
            pltpu.VMEM((n_rows * SIDE, line), f32),
            dma((len(LINKS), SLOTS - SPLIT)),
            dma((len(LINKS), SLOTS - SPLIT)),
            dma((SIDE - 1,)),
            dma((SIDE - 1,)),
            dma((2,)),
        ],
        compiler_params=pltpu.CompilerParams(
            collective_id=1, has_side_effects=True, vmem_limit_bytes=8 * 2**20
        ),
        name="finish",
    )(*pin(pltpu.VMEM, whole, lines, token))
    out_query, out_key, out_value, out_norm = pl.pallas_call(
        write_rest_kernel,
        out_shape=(*outs, shape(norm.shape, dtype)),
        in_specs=[vmem] * 3 + [anywhere] * 3,
        out_specs=[anywhere] * 4,
        input_output_aliases={3: 0, 4: 1, 5: 2},
        scratch_shapes=[dma((len(PIECES), 2)), dma(())],
        compiler_params=pltpu.CompilerParams(vmem_limit_bytes=4 * 2**20),
        name="write_rest",
    )(*pin(pltpu.VMEM, whole, rest, norm), *pin(pltpu.HBM, out_query, out_key, out_value))
    return out_query, out_key, out_value, out_norm.reshape(-1)


def solution(mesh):
    return jax.shard_map(
        body,
        mesh=mesh,
        in_specs=(
            P("rows", "cols"),
            P("rows", None),
            P(None, "cols"),
            P("rows", "cols"),
            P("rows", None),
            P(None, "cols"),
            P("rows", "cols"),
            P("rows", None),
            P(None, "cols"),
            P(("rows", "cols")),
            P(("rows", "cols")),
        ),
        out_specs=(P("cols", None), P("cols", None), P("cols", None), P()),
        check_vma=False,
    )
```

time: 191 us -> 116 us (0.61)
  the two profiles are of different devices: /device:TPU:1 before, /device:TPU:32 now
where the time goes in v2:
time: 116 us
  Pallas kernels  116 us (100%)
    pallas_call x1, Pallas kernels, body(): pl.pallas_call(gather_kernel, out_shape=(shape((n_rows, QUARTERS, unit, d...  99.8 us
    pallas_call x1, Pallas kernels, body(): pl.pallas_call(write_rest_kernel, out_shape=(*outs, shape(norm.shape, dty...  7.56 us
    pallas_call x1, Pallas kernels, body(): pl.pallas_call(finish_kernel, out_shape=(shape((len(LINKS), SLOTS - SPLIT...  7.12 us

profile of v2, /device:TPU:32, one launch (start us, length us, event | category | flops | bytes accessed | tf_op | source)
XLA Modules:
  0.0 116.3 jit_solution(17592348224310069088)
XLA Ops:
  0.6 99.8 %gather.1 = (bf16[16,4,288,512]{3,2,1,0:T(8,128)(2,1)S(1)}, f32[16,128]{1,0:T(8,128)S(1)}) custom-call(bf16[512,1024]{1,0:T(8,128)(2,1)} %train_query.1, bf16[64,512]{1,0:T(8,128)(2,1)} %bitcast.8, bf16[64,1024]{1,0:T(8,128)(2,1)} %high_query.1, bf16[64,512]{1,0:T(8,128)(2,1)} %bitcast.9, bf16[64,512]{1,0:T(8,128)(2,1)} %bitcast.10, ...), custom_call_target="tpu_custom_call" | custom-call | tf_op jit(solution)/shard_map/gather/pallas_call | solution.py:413
  100.4 1.2 %write.1 = (bf16[1024,8192]{1,0:T(8,128)(2,1)}, bf16[64,8192]{1,0:T(8,128)(2,1)}, bf16[64,8192]{1,0:T(8,128)(2,1)}, f32[8,128]{1,0:T(8,128)S(1)}) custom-call(bf16[16,4,288,512]{3,2,1,0:T(8,128)(2,1)S(1)} %get-tuple-element.16.whole), custom_call_target="tpu_custom_call" | custom-call | tf_op jit(solution)/shard_map/write/pallas_call | solution.py:452
  101.6 7.1 %finish.1 = (bf16[4,3,288,512]{3,2,1,0:T(8,128)(2,1)S(1)}, bf16[64,128]{1,0:T(8,128)(2,1)S(1)}) custom-call(bf16[16,4,288,512]{3,2,1,0:T(8,128)(2,1)S(1)} %get-tuple-element.16.whole, f32[16,128]{1,0:T(8,128)S(1)} %get-tuple-element.17.lines, f32[8,128]{1,0:T(8,128)S(1)} %get-tuple-element.18.token), custom_call_target="tpu_custom_call" | custom-call | tf_op jit(solution)/shard_map/finish/pallas_call | solution.py:461
  108.7 7.6 %write_rest.1 = (bf16[1024,8192]{1,0:T(8,128)(2,1)}, bf16[64,8192]{1,0:T(8,128)(2,1)}, bf16[64,8192]{1,0:T(8,128)(2,1)}, bf16[64,128]{1,0:T(8,128)(2,1)}) custom-call(bf16[16,4,288,512]{3,2,1,0:T(8,128)(2,1)S(1)} %get-tuple-element.16.whole, ...), custom_call_target="tpu_custom_call", output_to_operand_aliasing={{0}: (3, {}), {1}: (4, {}), {2}: (5, {})} | custom-call | tf_op jit(solution)/shard_map/write_rest/pallas_call | solution.py:483

commit v3 on v0

v3 whole, which is shorter than its diff:
```python
import jax
import jax.numpy as jnp
from jax import lax
from jax.experimental import pallas as pl
from jax.experimental.pallas import tpu as pltpu
from jax.sharding import PartitionSpec as P

MESH = pl.DeviceIdType.MESH

SIDE = 4
QUARTERS = 4
CORES = 2
LINKS = ((0, 1), (0, -1), (1, 0), (-1, 0))
ORDER = (0, 2, 1, 3)


def shift(off, d, sign=1):
    return ((off[0] + sign * d[0]) % SIDE, (off[1] + sign * d[1]) % SIDE)


def sends_of(link):
    d = LINKS[link]
    along_y = d[0] == 0
    first = (0, 1) if along_y else (2, 3)
    second = (2, 3) if along_y else (0, 1)
    positive = sum(d) > 0
    fwd_first = first[0] if positive else first[1]
    fwd_second = second[0] if positive else second[1]

    def across(n):
        return (n % SIDE, 0) if along_y else (0, n % SIDE)

    def behind(off):
        return shift(off, d, -1)

    own = (0, 0)
    return tuple((own, q) for q in ORDER) + (
        (behind(own), fwd_first),
        (across(-1), second[0]),
        (across(1), second[0]),
        (across(-1), second[1]),
        (across(1), second[1]),
        (behind(own), fwd_second),
        (across(2), second[0]),
        (across(2), second[1]),
        (behind(across(-1)), fwd_second),
        (behind(across(1)), fwd_second),
        (behind(across(2)), fwd_second),
    )


SENDS = tuple(sends_of(link) for link in range(len(LINKS)))
SLOTS = len(SENDS[0])
UNITS = [(link, slot) for slot in range(SLOTS) for link in range(len(LINKS))]


def arriving(link, slot):
    off, quarter = SENDS[link][slot]
    return shift(off, LINKS[link], -1), quarter


ARRIVES = {arriving(*unit): unit for unit in UNITS}
assert len(ARRIVES) == len(UNITS) == (SIDE * SIDE - 1) * QUARTERS
PASSED = []
for _link, _slot in UNITS:
    _what = SENDS[_link][_slot]
    if _what[0] != (0, 0) and ARRIVES[_what] not in PASSED:
        PASSED.append(ARRIVES[_what])
KEPT = [unit for unit in UNITS if unit not in PASSED]
assert len(KEPT) % QUARTERS == 0


class Place:
    def __init__(self):
        self.row, self.col = lax.axis_index("rows"), lax.axis_index("cols")
        self.z, self.y = self.row // SIDE, self.row % SIDE
        self.x, self.core = self.col // CORES, self.col % CORES

    def at(self, off):
        return ((self.z + off[0]) % SIDE) * SIDE + (self.y + off[1]) % SIDE

    def neighbour(self, d):
        return (self.at(d), self.col)

    def partner(self):
        return (self.row, self.x * CORES + 1 - self.core)

    def along_x(self, n):
        return (self.row, ((self.x + n) % SIDE) * CORES + self.core)


def remote(src, dst, send_sem, recv_sem, device):
    return pltpu.make_async_remote_copy(
        src_ref=src, dst_ref=dst, send_sem=send_sem, recv_sem=recv_sem, device_id=device, device_id_type=MESH
    )


def signal_all(barrier, devices):
    for device in devices:
        pl.semaphore_signal(barrier, inc=1, device_id=device, device_id_type=MESH)


def gather_kernel(
    train_query, low_query, high_query,
    train_key, low_key, high_key,
    train_value, low_value, high_value,
    norm_train, norm_step,
    whole, norm,
    tq, lq, hq, tk, lk, hk, tv, lv, hv, nt, ns, pair, ring, lines, all_lines, ordered,
    load_sem, send_sem, recv_sem, kept_sem, pair_sem, ring_send, ring_recv, line_sem, norm_send, norm_recv,
):
    me = Place()
    wide = tq.shape[1]
    part = wide // QUARTERS
    blocks = whole.shape[0]
    leader = (me.z == 0) & (me.y == 0)
    steps = range(1, SIDE)

    barrier = pltpu.get_barrier_semaphore()
    peers = [me.neighbour(d) for d in LINKS] + [me.partner()]
    signal_all(barrier, peers)

    @pl.when(leader)
    def _():
        signal_all(barrier, [me.along_x(n) for n in steps])

    loads = {}

    def load(name, src, dst):
        copy = pltpu.make_async_copy(src, dst, load_sem.at[len(loads)])
        copy.start()
        loads[name] = copy

    pieces = [(ORDER[0], 0, part // 2), (ORDER[0], part // 2, part)] + [(q, 0, part) for q in ORDER[1:]]
    load("lq", low_query, lq)
    load("hq", high_query, hq)
    for n, (q, start, end) in enumerate(pieces):
        cols = pl.ds(q * part + start, end - start)
        load(n, train_query.at[:, cols], tq.at[:, cols])
        if n == 1:
            load("tk", train_key, tk)
            load("lk", low_key, lk)
            load("hk", high_key, hk)
        if n == 2:
            load("tv", train_value, tv)
            load("lv", low_value, lv)
            load("hv", high_value, hv)
    load("nt", norm_train, nt)
    load("ns", norm_step, ns)

    def merged(train, high, low):
        return train.astype(jnp.float32) + lax.dot_general(
            high, low, (((0,), (0,)), ((), ())), preferred_element_type=jnp.float32
        )

    def unit_copy(link, slot, what, rows=slice(None)):
        off, q = what
        unit = whole.at[me.at(off), q, rows]
        sem = recv_sem.at[PASSED.index((link, slot))] if (link, slot) in PASSED else kept_sem
        return remote(unit, unit, send_sem, sem, me.neighbour(LINKS[link]))

    def send(link, slot, rows=slice(None)):
        unit_copy(link, slot, SENDS[link][slot], rows).start()

    arrived = set()

    def arrive(unit):
        if unit not in arrived:
            arrived.add(unit)
            unit_copy(*unit, arriving(*unit)).wait_recv()

    loads["lq"].wait()
    loads["hq"].wait()
    for n, (q, start, end) in enumerate(pieces):
        cols = pl.ds(q * part + start, end - start)
        loads[n].wait()
        whole[me.row, q, start:end, :] = merged(tq[:, cols].T, hq[:, cols], lq[...]).astype(whole.dtype)
        if n == 0:

            @pl.when(leader)
            def _():
                pl.semaphore_wait(barrier, len(peers) + len(steps))

            @pl.when(jnp.logical_not(leader))
            def _():
                pl.semaphore_wait(barrier, len(peers))

        if end == part:
            if n == 1:
                for name in ("tk", "lk", "hk"):
                    loads[name].wait()
            if n == 2:
                for name in ("tv", "lv", "hv"):
                    loads[name].wait()
            train, low, high = (tk, lk, hk) if q < 2 else (tv, lv, hv)
            small = merged(train[...], high[...], low[...]).astype(whole.dtype)
            half = small.shape[0] // 2
            whole[me.row, q, part:, :] = small[(q % 2) * half : (q % 2 + 1) * half, :]
        for link in range(len(LINKS)):
            if n == 0:
                send(link, 0, pl.ds(0, end))
            elif n == 1:
                send(link, 0, pl.ds(start, whole.shape[2] - start))
            else:
                send(link, ORDER.index(q))

    loads["nt"].wait()
    loads["ns"].wait()
    fresh = nt[...] + ns[...]
    pair[me.core] = jnp.concatenate([fresh, fresh], axis=1)

    def pair_copy(slot):
        return remote(pair.at[slot], pair.at[slot], pair_sem.at[0], pair_sem.at[1], me.partner())

    pair_copy(me.core).start()

    def ring_copy(n, src, d):
        return remote(src, src, ring_send, ring_recv.at[n], me.neighbour(d))

    def column(dz):
        return ring.at[pl.ds(((me.z + dz) % SIDE) * SIDE, SIDE)]

    def line_copy(n):
        return remote(lines, all_lines.at[me.x], line_sem.at[0], line_sem.at[1], me.along_x(n))

    def norm_copy(link):
        return remote(norm, norm, norm_send.at[link], norm_recv, me.neighbour(LINKS[link]))

    passes = [((0, 0), (0, 1, 2, 3)), ((0, 1), (0, 2, 3)), ((0, 3), (2, 3)), ((0, 2), (2, 3))]
    passes += [((1, y), (2,)) for y in range(SIDE)]

    def pass_norm(places):
        for (z, y), links in passes:
            if (z, y) in places:

                @pl.when((me.z == z) & (me.y == y))
                def _():
                    if (z, y) != (0, 0):
                        norm_copy(0).wait_recv()
                    for link in links:
                        norm_copy(link).start()

    def norm_step_of(step):
        if step == 0:
            pair_copy(1 - me.core).wait_recv()
            lane = lax.broadcasted_iota(jnp.int32, (1, pair.shape[2]), 1)
            ring[me.row] = jnp.where(lane < pair.shape[2] // CORES, pair[0], pair[1])
        if step == 1:
            ring_copy(0, ring.at[me.row], (0, 1)).start()
            ring_copy(1, ring.at[me.row], (0, -1)).start()
        if step == 2:
            ring_copy(0, ring.at[me.at((0, -1))], (0, 1)).wait_recv()
            ring_copy(1, ring.at[me.at((0, 1))], (0, -1)).wait_recv()
            ring_copy(2, ring.at[me.at((0, -1))], (0, 1)).start()
        if step == 3:
            ring_copy(2, ring.at[me.at((0, -2))], (0, 1)).wait_recv()
            ring_copy(3, column(0), (1, 0)).start()
            ring_copy(4, column(0), (-1, 0)).start()
        if step == 4:
            ring_copy(3, column(-1), (1, 0)).wait_recv()
            ring_copy(4, column(1), (-1, 0)).wait_recv()
            ring_copy(5, column(-1), (1, 0)).start()
        if step == 5:
            ring_copy(5, column(-2), (1, 0)).wait_recv()

            @pl.when(leader)
            def _():
                lines[...] = jnp.concatenate([ring[i] for i in range(blocks)], axis=0)
                all_lines[me.x] = lines[...]
                for n in steps:
                    line_copy(n).start()

        if step == 7:

            @pl.when(leader)
            def _():
                three = all_lines.at[pl.ds(0, len(steps))]
                every = remote(three, three, line_sem.at[0], line_sem.at[1], me.along_x(1))
                every.wait_recv()
                for x in range(SIDE):
                    ordered[pl.Slice(x, blocks, SIDE), :] = all_lines[x]
                norm[...] = ordered[...].astype(norm.dtype)

            pass_norm([(0, 0)])
        if step == 8:
            pass_norm([(0, 1), (0, 3)])
        if step == 9:
            pass_norm([(0, 2)])
        if step == 10:
            pass_norm([(1, y) for y in range(SIDE)])

    for slot in range(QUARTERS, SLOTS):
        for link in range(len(LINKS)):
            arrive(ARRIVES[SENDS[link][slot]])
            send(link, slot)
        norm_step_of(slot - QUARTERS)

    @pl.when(me.z >= 2)
    def _():
        norm_copy(0).wait_recv()

    for unit in PASSED:
        arrive(unit)
    kept = whole.at[pl.ds(0, len(KEPT) // QUARTERS)]
    remote(kept, kept, send_sem, kept_sem, me.partner()).wait_recv()
    sent = whole.at[pl.ds(0, len(UNITS) // QUARTERS)]
    remote(sent, sent, send_sem, kept_sem, me.partner()).wait_send()
    pair_copy(me.core).wait_send()
    around = ring.at[pl.ds(0, blocks - 1)]
    remote(around, around, ring_send, ring_recv.at[0], me.partner()).wait_send()

    @pl.when(leader)
    def _():
        three = all_lines.at[pl.ds(0, len(steps))]
        remote(three, three, line_sem.at[0], line_sem.at[1], me.along_x(1)).wait_send()

    for (z, y), links in passes:

        @pl.when((me.z == z) & (me.y == y))
        def _():
            for link in links:
                norm_copy(link).wait_send()


def write_kernel(whole, norm, out_query, out_key, out_value, out_norm, sem):
    blocks, quarters, rows, depth = whole.shape
    part = out_query.shape[0] // quarters
    half = rows - part
    outs = (out_query, out_key, out_value, out_norm)
    pltpu.make_async_copy(norm, out_norm, sem.at[3]).start()

    @pl.loop(0, blocks)
    def _(r):
        at = pl.ds(pl.multiple_of(r * depth, depth), depth)
        for q in range(quarters):
            pltpu.make_async_copy(
                whole.at[r, q, pl.ds(0, part)], out_query.at[pl.ds(q * part, part), at], sem.at[0]
            ).start()
        for q in range(quarters):
            n = 1 + q // 2
            pltpu.make_async_copy(
                whole.at[r, q, pl.ds(part, half)], outs[n].at[pl.ds((q % 2) * half, half), at], sem.at[n]
            ).start()

    for n, out in enumerate(outs):
        pltpu.make_async_copy(out, out, sem.at[n]).wait()


def body(
    train_query, low_query, high_query,
    train_key, low_key, high_key,
    train_value, low_value, high_value,
    norm_train, norm_step,
):
    n_rows, n_cols = lax.axis_size("rows"), lax.axis_size("cols")
    depth, wide = train_query.shape
    tall = train_key.shape[1]
    rank = low_query.shape[1]
    unit = (wide + 2 * tall) // QUARTERS
    values = norm_train.shape[0]
    line = CORES * values
    dtype = train_query.dtype
    f32 = jnp.float32
    anywhere = pl.BlockSpec(memory_space=pl.ANY)
    vmem = pl.BlockSpec(memory_space=pltpu.VMEM)
    dma = pltpu.SemaphoreType.DMA
    shape = jax.ShapeDtypeStruct

    def pin(space, *arrays):
        return [pltpu.with_memory_space_constraint(a, space) for a in arrays]

    whole, norm = pl.pallas_call(
        gather_kernel,
        out_shape=(
            shape((n_rows, QUARTERS, unit, depth), dtype),
            shape((n_rows * n_cols // CORES, line), dtype),
        ),
        in_specs=[anywhere] * 11,
        out_specs=(vmem, vmem),
        scratch_shapes=[
            pltpu.VMEM((depth, wide), dtype),
            pltpu.VMEM((rank, depth), dtype),
            pltpu.VMEM((rank, wide), dtype),
            pltpu.VMEM((tall, depth), dtype),
            pltpu.VMEM((rank, depth), dtype),
            pltpu.VMEM((rank, tall), dtype),
            pltpu.VMEM((tall, depth), dtype),
            pltpu.VMEM((rank, depth), dtype),
            pltpu.VMEM((rank, tall), dtype),
            pltpu.VMEM((1, values), f32),
            pltpu.VMEM((1, values), f32),
            pltpu.VMEM((CORES, 1, line), f32),
            pltpu.VMEM((n_rows, 1, line), f32),
            pltpu.VMEM((n_rows, line), f32),
            pltpu.VMEM((SIDE, n_rows, line), f32),
            pltpu.VMEM((SIDE * n_rows, line), f32),
            dma((15,)),
            dma(()),
            dma((len(PASSED),)),
            dma(()),
            dma((2,)),
            dma(()),
            dma((6,)),
            dma((2,)),
            dma((len(LINKS),)),
            dma(()),
        ],
        compiler_params=pltpu.CompilerParams(
            collective_id=0, has_side_effects=True, vmem_limit_bytes=24 * 2**20
        ),
        name="gather",
    )(
        *pin(
            pltpu.HBM,
            train_query, low_query.T, high_query,
            train_key.T, low_key.T, high_key,
            train_value.T, low_value.T, high_value,
            norm_train.reshape(1, -1), norm_step.reshape(1, -1),
        )
    )
    out_query, out_key, out_value, out_norm = pl.pallas_call(
        write_kernel,
        out_shape=(
            shape((wide, n_rows * depth), dtype),
            shape((tall, n_rows * depth), dtype),
            shape((tall, n_rows * depth), dtype),
            shape(norm.shape, dtype),
        ),
        in_specs=[vmem] * 2,
        out_specs=[anywhere] * 4,
        scratch_shapes=[dma((4,))],
        compiler_params=pltpu.CompilerParams(vmem_limit_bytes=4 * 2**20),
        name="write",
    )(*pin(pltpu.VMEM, whole, norm))
    return out_query, out_key, out_value, out_norm.reshape(-1)


def solution(mesh):
    return jax.shard_map(
        body,
        mesh=mesh,
        in_specs=(
            P("rows", "cols"),
            P("rows", None),
            P(None, "cols"),
            P("rows", "cols"),
            P("rows", None),
            P(None, "cols"),
            P("rows", "cols"),
            P("rows", None),
            P(None, "cols"),
            P(("rows", "cols")),
            P(("rows", "cols")),
        ),
        out_specs=(P("cols", None), P("cols", None), P("cols", None), P()),
        check_vma=False,
    )
```

time: 191 us -> 110 us (0.58)
  Pallas kernels: 0 us -> 109 us
  blocking collectives: 71.5 us -> 0 us
  waiting for transfers between devices: 54.5 us -> 0 us
  local copies, waits for them, and re-layouts: 46.4 us -> 0 us
  between operations: 14.1 us -> 0.64 us
  matrix products: 3.93 us -> 0 us
    pallas_call x0 -> x2, Pallas kernels: none -> 109 us  [the longest x1 103 us: body(): pl.pallas_call(gather_kernel, out_shape=(shape((n_rows, QUARTERS, unit, d...]
    unnamed x1 -> x0, blocking collectives: 71.5 us -> none
    all_gather x1 -> x0, waiting for transfers between devices: 54.5 us -> none  [side_by_side(): lax.all_gather(both, axis, axis=dim, tiled=True)]
    unnamed x11 -> x0, local copies, waits for them, and re-layouts: 25.8 us -> none
    transpose x2 -> x0, local copies, waits for them, and re-layouts: 18.4 us -> none  [body(): serving_query, serving_key, serving_value = (serving_query.T, serving_key...]
    dot_general x3 -> x0, matrix products: 3.93 us -> none  [the longest x1 1.72 us: body(): jnp.dot(low_query, high_query, preferred_element_type=jnp.float32)]
    concatenate x1 -> x0, local copies, waits for them, and re-layouts: 1.93 us -> none  [side_by_side(): both = jnp.concatenate(arrays, axis=along)]
  transfers between devices with their start and end apart: 1 -> 0, of which waited for: 1 -> 0; matrix products, arithmetic and copies ran while one was open for 0% -> 0% of each run, Pallas kernels for 0% -> 0%
where the time goes in v3:
time: 110 us
  Pallas kernels  109 us (99%)
    pallas_call x1, Pallas kernels, body(): pl.pallas_call(gather_kernel, out_shape=(shape((n_rows, QUARTERS, unit, d...  103 us
    pallas_call x1, Pallas kernels, body(): pl.pallas_call(write_kernel, out_shape=(shape((wide, n_rows * depth), dty...  6.4 us

profile of v3, /device:TPU:1, one launch (start us, length us, event | category | flops | bytes accessed | tf_op | source)
XLA Modules:
  0.0 109.9 jit_solution(9436425727726615768)
XLA Ops:
  0.6 102.9 %gather.1 = (bf16[16,4,288,512]{3,2,1,0:T(8,128)(2,1)S(1)}, bf16[64,128]{1,0:T(8,128)(2,1)S(1)}) custom-call(bf16[512,1024]{1,0:T(8,128)(2,1)} %train_query.1, bf16[64,512]{1,0:T(8,128)(2,1)} %bitcast.8, bf16[64,1024]{1,0:T(8,128)(2,1)} %high_query.1, bf16[64,512]{1,0:T(8,128)(2,1)} %bitcast.9, bf16[64,512]{1,0:T(8,128)(2,1)} %bitcast.10, ...), custom_call_target="tpu_custom_call" | custom-call | tf_op jit(solution)/shard_map/gather/pallas_call | solution.py:372
  103.5 6.4 %write.1 = (bf16[1024,8192]{1,0:T(8,128)(2,1)}, bf16[64,8192]{1,0:T(8,128)(2,1)}, bf16[64,8192]{1,0:T(8,128)(2,1)}, bf16[64,128]{1,0:T(8,128)(2,1)}) custom-call(bf16[16,4,288,512]{3,2,1,0:T(8,128)(2,1)S(1)} %get-tuple-element.10.whole, bf16[64,128]{1,0:T(8,128)(2,1)S(1)} %get-tuple-element.11.norm), custom_call_target="tpu_custom_call" | custom-call | tf_op jit(solution)/shard_map/write/pallas_call | solution.py:421

commit v4 on v3

--- a/solution.py
+++ b/solution.py
@@ -11,6 +11,7 @@
 QUARTERS = 4
 CORES = 2
 LINKS = ((0, 1), (0, -1), (1, 0), (-1, 0))
+LEADER = 2
 ORDER = (0, 2, 1, 3)
 
 
@@ -113,7 +114,7 @@
     wide = tq.shape[1]
     part = wide // QUARTERS
     blocks = whole.shape[0]
-    leader = (me.z == 0) & (me.y == 0)
+    leader = (me.z == LEADER) & (me.y == LEADER)
     steps = range(1, SIDE)
 
     barrier = pltpu.get_barrier_semaphore()
@@ -226,6 +227,7 @@
     def norm_copy(link):
         return remote(norm, norm, norm_send.at[link], norm_recv, me.neighbour(LINKS[link]))
 
+    from_leader = ((me.z - LEADER) % SIDE, (me.y - LEADER) % SIDE)
     passes = [((0, 0), (0, 1, 2, 3)), ((0, 1), (0, 2, 3)), ((0, 3), (2, 3)), ((0, 2), (2, 3))]
     passes += [((1, y), (2,)) for y in range(SIDE)]
 
@@ -233,7 +235,7 @@
         for (z, y), links in passes:
             if (z, y) in places:
 
-                @pl.when((me.z == z) & (me.y == y))
+                @pl.when((from_leader[0] == z) & (from_leader[1] == y))
                 def _():
                     if (z, y) != (0, 0):
                         norm_copy(0).wait_recv()
@@ -295,7 +297,7 @@
             send(link, slot)
         norm_step_of(slot - QUARTERS)
 
-    @pl.when(me.z >= 2)
+    @pl.when(from_leader[0] >= 2)
     def _():
         norm_copy(0).wait_recv()
 
@@ -316,7 +318,7 @@
 
     for (z, y), links in passes:
 
-        @pl.when((me.z == z) & (me.y == y))
+        @pl.when((from_leader[0] == z) & (from_leader[1] == y))
         def _():
             for link in links:
                 norm_copy(link).wait_send()

time: 110 us -> 111 us (level)
  no operation moved by 1% of the time
where the time goes in v4:
time: 111 us; the launch traced here: 110 us
  Pallas kernels  110 us (99%)
    pallas_call x1, Pallas kernels, body(): pl.pallas_call(gather_kernel, out_shape=(shape((n_rows, QUARTERS, unit, d...  103 us
    pallas_call x1, Pallas kernels, body(): pl.pallas_call(write_kernel, out_shape=(shape((wide, n_rows * depth), dty...  6.4 us

profile of v4, /device:TPU:1, one launch (start us, length us, event | category | flops | bytes accessed | tf_op | source)
XLA Modules:
  0.0 110.3 jit_solution(17018257823316553482)
XLA Ops:
  0.6 103.2 %gather.1 = (bf16[16,4,288,512]{3,2,1,0:T(8,128)(2,1)S(1)}, bf16[64,128]{1,0:T(8,128)(2,1)S(1)}) custom-call(bf16[512,1024]{1,0:T(8,128)(2,1)} %train_query.1, bf16[64,512]{1,0:T(8,128)(2,1)} %bitcast.8, bf16[64,1024]{1,0:T(8,128)(2,1)} %high_query.1, bf16[64,512]{1,0:T(8,128)(2,1)} %bitcast.9, bf16[64,512]{1,0:T(8,128)(2,1)} %bitcast.10, ...), custom_call_target="tpu_custom_call" | custom-call | tf_op jit(solution)/shard_map/gather/pallas_call | solution.py:374
  103.9 6.4 %write.1 = (bf16[1024,8192]{1,0:T(8,128)(2,1)}, bf16[64,8192]{1,0:T(8,128)(2,1)}, bf16[64,8192]{1,0:T(8,128)(2,1)}, bf16[64,128]{1,0:T(8,128)(2,1)}) custom-call(bf16[16,4,288,512]{3,2,1,0:T(8,128)(2,1)S(1)} %get-tuple-element.10.whole, bf16[64,128]{1,0:T(8,128)(2,1)S(1)} %get-tuple-element.11.norm), custom_call_target="tpu_custom_call" | custom-call | tf_op jit(solution)/shard_map/write/pallas_call | solution.py:423

commit v5 on v3

--- a/solution.py
+++ b/solution.py
@@ -11,6 +11,8 @@
 QUARTERS = 4
 CORES = 2
 LINKS = ((0, 1), (0, -1), (1, 0), (-1, 0))
+LATE = 1
+SPLIT = 12
 ORDER = (0, 2, 1, 3)
 
 
@@ -35,9 +37,9 @@
 
     own = (0, 0)
     return tuple((own, q) for q in ORDER) + (
-        (behind(own), fwd_first),
         (across(-1), second[0]),
         (across(1), second[0]),
+        (behind(own), fwd_first),
         (across(-1), second[1]),
         (across(1), second[1]),
         (behind(own), fwd_second),
@@ -61,13 +63,15 @@
 
 ARRIVES = {arriving(*unit): unit for unit in UNITS}
 assert len(ARRIVES) == len(UNITS) == (SIDE * SIDE - 1) * QUARTERS
-PASSED = []
-for _link, _slot in UNITS:
-    _what = SENDS[_link][_slot]
-    if _what[0] != (0, 0) and ARRIVES[_what] not in PASSED:
-        PASSED.append(ARRIVES[_what])
-KEPT = [unit for unit in UNITS if unit not in PASSED]
-assert len(KEPT) % QUARTERS == 0
+LAST = [unit for unit in UNITS if unit[1] >= SPLIT]
+GROUPS = ((0, 1), (2, 3), (6,), (4, 5, 7, 8), (10, 11), (9,), (12, 13, 14))
+GROUP_OF = {slot: group for group, slots in enumerate(GROUPS) for slot in slots}
+assert sorted(GROUP_OF) == list(range(SLOTS)) and GROUPS[-1] == tuple(range(SPLIT, SLOTS))
+AFTER = ((4, 5), (6, 7, 8, 9), (10, 11), (12, 13), (14,))
+for _group, _slots in enumerate(AFTER):
+    for _slot in _slots:
+        for _link in range(len(LINKS)):
+            assert GROUP_OF[ARRIVES[SENDS[_link][_slot]][1]] <= _group
 
 
 class Place:
@@ -107,7 +111,7 @@
     norm_train, norm_step,
     whole, norm,
     tq, lq, hq, tk, lk, hk, tv, lv, hv, nt, ns, pair, ring, lines, all_lines, ordered,
-    load_sem, send_sem, recv_sem, kept_sem, pair_sem, ring_send, ring_recv, line_sem, norm_send, norm_recv,
+    load_sem, send_sem, recv_sem, pair_sem, ring_send, ring_recv, line_sem, norm_send, norm_recv,
 ):
     me = Place()
     wide = tq.shape[1]
@@ -156,18 +160,20 @@
     def unit_copy(link, slot, what, rows=slice(None)):
         off, q = what
         unit = whole.at[me.at(off), q, rows]
-        sem = recv_sem.at[PASSED.index((link, slot))] if (link, slot) in PASSED else kept_sem
-        return remote(unit, unit, send_sem, sem, me.neighbour(LINKS[link]))
+        return remote(unit, unit, send_sem, recv_sem.at[GROUP_OF[slot]], me.neighbour(LINKS[link]))
 
     def send(link, slot, rows=slice(None)):
         unit_copy(link, slot, SENDS[link][slot], rows).start()
 
-    arrived = set()
-
-    def arrive(unit):
-        if unit not in arrived:
-            arrived.add(unit)
-            unit_copy(*unit, arriving(*unit)).wait_recv()
+    def units(slots, sem):
+        some = whole.at[pl.ds(0, slots * len(LINKS) // QUARTERS)]
+        return remote(some, some, send_sem, sem, me.partner())
+
+    def arrive(group):
+        units(len(GROUPS[group]), recv_sem.at[group]).wait_recv()
+
+    def only(core):
+        return pl.when(me.core == LATE if core == LATE else me.core != LATE)
 
     loads["lq"].wait()
     loads["hq"].wait()
@@ -289,22 +295,41 @@
         if step == 10:
             pass_norm([(1, y) for y in range(SIDE)])
 
-    for slot in range(QUARTERS, SLOTS):
-        for link in range(len(LINKS)):
-            arrive(ARRIVES[SENDS[link][slot]])
-            send(link, slot)
-        norm_step_of(slot - QUARTERS)
-
-    @pl.when(me.z >= 2)
-    def _():
-        norm_copy(0).wait_recv()
-
-    for unit in PASSED:
-        arrive(unit)
-    kept = whole.at[pl.ds(0, len(KEPT) // QUARTERS)]
-    remote(kept, kept, send_sem, kept_sem, me.partner()).wait_recv()
-    sent = whole.at[pl.ds(0, len(UNITS) // QUARTERS)]
-    remote(sent, sent, send_sem, kept_sem, me.partner()).wait_send()
+    def send_slots(slots):
+        for slot in slots:
+            for link in range(len(LINKS)):
+                send(link, slot)
+
+    norm_steps = ((0, 1), (2, 3), (4, 5, 7), (8, 9, 10), ())
+    for group, slots in enumerate(AFTER):
+        arrive(group)
+        if slots[0] < SPLIT:
+            send_slots(slots)
+        else:
+
+            @only(1 - LATE)
+            def _():
+                send_slots(slots)
+
+        for step in norm_steps[group]:
+            norm_step_of(step)
+        if 10 in norm_steps[group]:
+
+            @pl.when(me.z >= 2)
+            def _():
+                norm_copy(0).wait_recv()
+
+    arrive(5)
+
+    @only(1 - LATE)
+    def _():
+        arrive(6)
+        units(SLOTS, recv_sem.at[0]).wait_send()
+
+    @only(LATE)
+    def _():
+        units(SPLIT, recv_sem.at[0]).wait_send()
+
     pair_copy(me.core).wait_send()
     around = ring.at[pl.ds(0, blocks - 1)]
     remote(around, around, ring_send, ring_recv.at[0], me.partner()).wait_send()
@@ -322,28 +347,89 @@
                 norm_copy(link).wait_send()
 
 
-def write_kernel(whole, norm, out_query, out_key, out_value, out_norm, sem):
-    blocks, quarters, rows, depth = whole.shape
-    part = out_query.shape[0] // quarters
+def finish_kernel(whole, token, rest, send_sem, recv_sem):
+    del token
+    me = Place()
+
+    @pl.when(me.core == LATE)
+    def _():
+        barrier = pltpu.get_barrier_semaphore()
+        signal_all(barrier, [me.neighbour(d) for d in LINKS])
+        pl.semaphore_wait(barrier, len(LINKS))
+        for link, slot in LAST:
+            off, q = SENDS[link][slot]
+            unit = whole.at[me.at(off), q]
+            remote(unit, rest.at[link, slot - SPLIT], send_sem, recv_sem, me.neighbour(LINKS[link])).start()
+        remote(rest, rest, send_sem, recv_sem, me.partner()).wait()
+
+
+def write_unit(source, block, quarter, outs, sems):
+    out_query, out_key, out_value = outs
+    rows, depth = source.shape
+    part = out_query.shape[0] // QUARTERS
     half = rows - part
-    outs = (out_query, out_key, out_value, out_norm)
-    pltpu.make_async_copy(norm, out_norm, sem.at[3]).start()
-
-    @pl.loop(0, blocks)
-    def _(r):
-        at = pl.ds(pl.multiple_of(r * depth, depth), depth)
-        for q in range(quarters):
-            pltpu.make_async_copy(
-                whole.at[r, q, pl.ds(0, part)], out_query.at[pl.ds(q * part, part), at], sem.at[0]
-            ).start()
-        for q in range(quarters):
-            n = 1 + q // 2
-            pltpu.make_async_copy(
-                whole.at[r, q, pl.ds(part, half)], outs[n].at[pl.ds((q % 2) * half, half), at], sem.at[n]
-            ).start()
-
-    for n, out in enumerate(outs):
-        pltpu.make_async_copy(out, out, sem.at[n]).wait()
+    at = pl.ds(pl.multiple_of(block * depth, depth), depth)
+    small = (out_key if quarter < 2 else out_value).at[pl.ds((quarter % 2) * half, half), at]
+    pltpu.make_async_copy(source.at[pl.ds(0, part)], out_query.at[pl.ds(quarter * part, part), at], sems[0]).start()
+    pltpu.make_async_copy(source.at[pl.ds(part, half)], small, sems[1 + quarter // 2]).start()
+
+
+def wait_units(count, unit_bytes, out, sem):
+    rows = count * unit_bytes // (out.shape[1] * out.dtype.itemsize)
+    same = out.at[pl.ds(0, rows)]
+    pltpu.make_async_copy(same, same, sem).wait()
+
+
+def unit_bytes_of(whole):
+    return whole.shape[-2] * whole.shape[-1] * whole.dtype.itemsize
+
+
+def write_kernel(whole, out_query, out_key, out_value, token, sem):
+    me = Place()
+    outs = (out_query, out_key, out_value)
+    token[...] = jnp.zeros_like(token)
+    late = {arriving(*unit) for unit in LAST}
+
+    @pl.when(me.core == LATE)
+    def _():
+        count = 0
+        for off in [(dz, dy) for dz in range(SIDE) for dy in range(SIDE)]:
+            for q in range(QUARTERS):
+                if (off, q) not in late:
+                    count += 1
+                    block = me.at(off)
+                    write_unit(whole.at[block, q], block, q, outs, (sem, sem, sem))
+        wait_units(count, unit_bytes_of(whole), out_query, sem)
+
+
+def write_rest_kernel(
+    whole, rest, norm, in_query, in_key, in_value, out_query, out_key, out_value, out_norm, sem, norm_sem
+):
+    del in_query, in_key, in_value
+    me = Place()
+    outs = (out_query, out_key, out_value)
+    norm_copy = pltpu.make_async_copy(norm, out_norm, norm_sem)
+    norm_copy.start()
+
+    @pl.when(me.core == LATE)
+    def _():
+        first = sem.at[0]
+        for link, slot in LAST:
+            off, q = arriving(link, slot)
+            write_unit(rest.at[link, slot - SPLIT], me.at(off), q, outs, (first, first, first))
+        wait_units(len(LAST), unit_bytes_of(whole), out_query, first)
+
+    @pl.when(me.core != LATE)
+    def _():
+        @pl.loop(0, whole.shape[0])
+        def _(block):
+            for q in range(QUARTERS):
+                write_unit(whole.at[block, q], block, q, outs, [sem.at[n] for n in range(len(outs))])
+
+        for n, out in enumerate(outs):
+            pltpu.make_async_copy(out, out, sem.at[n]).wait()
+
+    norm_copy.wait()
 
 
 def body(
@@ -396,8 +482,7 @@
             pltpu.VMEM((SIDE * n_rows, line), f32),
             dma((15,)),
             dma(()),
-            dma((len(PASSED),)),
-            dma(()),
+            dma((len(GROUPS),)),
             dma((2,)),
             dma(()),
             dma((6,)),
@@ -418,20 +503,37 @@
             norm_train.reshape(1, -1), norm_step.reshape(1, -1),
         )
     )
-    out_query, out_key, out_value, out_norm = pl.pallas_call(
+    outs = [shape((wide, n_rows * depth), dtype)] + [shape((tall, n_rows * depth), dtype)] * 2
+    out_query, out_key, out_value, token = pl.pallas_call(
         write_kernel,
-        out_shape=(
-            shape((wide, n_rows * depth), dtype),
-            shape((tall, n_rows * depth), dtype),
-            shape((tall, n_rows * depth), dtype),
-            shape(norm.shape, dtype),
-        ),
-        in_specs=[vmem] * 2,
-        out_specs=[anywhere] * 4,
-        scratch_shapes=[dma((4,))],
+        out_shape=(*outs, shape((8, 128), f32)),
+        in_specs=[vmem],
+        out_specs=[anywhere] * 3 + [vmem],
+        scratch_shapes=[dma(())],
         compiler_params=pltpu.CompilerParams(vmem_limit_bytes=4 * 2**20),
         name="write",
-    )(*pin(pltpu.VMEM, whole, norm))
+    )(*pin(pltpu.VMEM, whole))
+    (rest,) = pl.pallas_call(
+        finish_kernel,
+        out_shape=(shape((len(LINKS), SLOTS - SPLIT, unit, depth), dtype),),
+        in_specs=[vmem] * 2,
+        out_specs=(vmem,),
+        scratch_shapes=[dma(()), dma(())],
+        compiler_params=pltpu.CompilerParams(
+            collective_id=1, has_side_effects=True, vmem_limit_bytes=8 * 2**20
+        ),
+        name="finish",
+    )(*pin(pltpu.VMEM, whole, token))
+    out_query, out_key, out_value, out_norm = pl.pallas_call(
+        write_rest_kernel,
+        out_shape=(*outs, shape(norm.shape, dtype)),
+        in_specs=[vmem] * 3 + [anywhere] * 3,
+        out_specs=[anywhere] * 4,
+        input_output_aliases={3: 0, 4: 1, 5: 2},
+        scratch_shapes=[dma((len(outs),)), dma(())],
+        compiler_params=pltpu.CompilerParams(vmem_limit_bytes=4 * 2**20),
+        name="write_rest",
+    )(*pin(pltpu.VMEM, whole, rest, norm), *pin(pltpu.HBM, out_query, out_key, out_value))
     return out_query, out_key, out_value, out_norm.reshape(-1)
 
 

time: 110 us -> 117 us (1.064); the launches traced: 110 us -> 116 us
  Pallas kernels: 109 us -> 115 us
    pallas_call x1 -> x3, Pallas kernels: 6.4 us -> 25.2 us  [the longest x1 18 us: body(): pl.pallas_call(finish_kernel, out_shape=(shape((len(LINKS), SLOTS - SPLIT...]
    pallas_call x1, Pallas kernels: 103 us -> 89.8 us  [body(): pl.pallas_call(gather_kernel, out_shape=(shape((n_rows, QUARTERS, unit, d...]
where the time goes in v5:
time: 117 us; the launch traced here: 116 us
  Pallas kernels  115 us (98%)
    pallas_call x1, Pallas kernels, body(): pl.pallas_call(gather_kernel, out_shape=(shape((n_rows, QUARTERS, unit, d...  89.8 us
    pallas_call x1, Pallas kernels, body(): pl.pallas_call(finish_kernel, out_shape=(shape((len(LINKS), SLOTS - SPLIT...  18 us
    pallas_call x1, Pallas kernels, body(): pl.pallas_call(write_kernel, out_shape=(*outs, shape((8, 128), f32)), in_...  5.35 us

profile of v5, /device:TPU:1, one launch (start us, length us, event | category | flops | bytes accessed | tf_op | source)
XLA Modules:
  0.0 115.6 jit_solution(3829226367454125786)
XLA Ops:
  0.6 89.8 %gather.1 = (bf16[16,4,288,512]{3,2,1,0:T(8,128)(2,1)S(1)}, bf16[64,128]{1,0:T(8,128)(2,1)S(1)}) custom-call(bf16[512,1024]{1,0:T(8,128)(2,1)} %train_query.1, bf16[64,512]{1,0:T(8,128)(2,1)} %bitcast.8, bf16[64,1024]{1,0:T(8,128)(2,1)} %high_query.1, bf16[64,512]{1,0:T(8,128)(2,1)} %bitcast.9, bf16[64,512]{1,0:T(8,128)(2,1)} %bitcast.10, ...), custom_call_target="tpu_custom_call" | custom-call | tf_op jit(solution)/shard_map/gather/pallas_call | solution.py:458
  90.4 5.3 %write.1 = (bf16[1024,8192]{1,0:T(8,128)(2,1)}, bf16[64,8192]{1,0:T(8,128)(2,1)}, bf16[64,8192]{1,0:T(8,128)(2,1)}, f32[8,128]{1,0:T(8,128)S(1)}) custom-call(bf16[16,4,288,512]{3,2,1,0:T(8,128)(2,1)S(1)} %get-tuple-element.14.whole), custom_call_target="tpu_custom_call" | custom-call | tf_op jit(solution)/shard_map/write/pallas_call | solution.py:507
  95.8 18.0 %finish.1.rest = bf16[4,3,288,512]{3,2,1,0:T(8,128)(2,1)S(1)} custom-call(bf16[16,4,288,512]{3,2,1,0:T(8,128)(2,1)S(1)} %get-tuple-element.14.whole, f32[8,128]{1,0:T(8,128)S(1)} %get-tuple-element.15.token), custom_call_target="tpu_custom_call" | custom-call | tf_op jit(solution)/shard_map/finish/pallas_call | solution.py:516
  113.8 1.8 %write_rest.1 = (bf16[1024,8192]{1,0:T(8,128)(2,1)}, bf16[64,8192]{1,0:T(8,128)(2,1)}, bf16[64,8192]{1,0:T(8,128)(2,1)}, bf16[64,128]{1,0:T(8,128)(2,1)}) custom-call(bf16[16,4,288,512]{3,2,1,0:T(8,128)(2,1)S(1)} %get-tuple-element.14.whole, bf16[4,3,288,512]{3,2,1,0:T(8,128)(2,1)S(1)} %finish.1.rest, ...), custom_call_target="tpu_custom_call", output_to_operand_aliasing={{0}: (3, {}), {1}: (4, {}), {2}: (5, {})} | custom-call | tf_op jit(solution)/shard_map/write_rest/pallas_call | solution.py:527

commit v6 on v5

--- a/solution.py
+++ b/solution.py
@@ -89,8 +89,8 @@
     def partner(self):
         return (self.row, self.x * CORES + 1 - self.core)
 
-    def along_x(self, n):
-        return (self.row, ((self.x + n) % SIDE) * CORES + self.core)
+    def plane(self, n):
+        return (self.row, (self.col + n) % (SIDE * CORES))
 
 
 def remote(src, dst, send_sem, recv_sem, device):
@@ -110,15 +110,16 @@
     train_value, low_value, high_value,
     norm_train, norm_step,
     whole, norm,
-    tq, lq, hq, tk, lk, hk, tv, lv, hv, nt, ns, pair, ring, lines, all_lines, ordered,
-    load_sem, send_sem, recv_sem, pair_sem, ring_send, ring_recv, line_sem, norm_send, norm_recv,
+    tq, lq, hq, tk, lk, hk, tv, lv, hv, nt, ns, fresh, ring, lines, ordered,
+    load_sem, send_sem, recv_sem, fresh_sem, line_sem, norm_sem,
 ):
     me = Place()
     wide = tq.shape[1]
     part = wide // QUARTERS
     blocks = whole.shape[0]
     leader = (me.z == 0) & (me.y == 0)
-    steps = range(1, SIDE)
+    n_planes = lines.shape[0]
+    others = [(dz, dy) for dz in range(SIDE) for dy in range(SIDE) if (dz, dy) != (0, 0)]
 
     barrier = pltpu.get_barrier_semaphore()
     peers = [me.neighbour(d) for d in LINKS] + [me.partner()]
@@ -126,7 +127,7 @@
 
     @pl.when(leader)
     def _():
-        signal_all(barrier, [me.along_x(n) for n in steps])
+        signal_all(barrier, [me.neighbour(off) for off in others] + [me.plane(n) for n in range(1, n_planes)])
 
     loads = {}
 
@@ -136,6 +137,8 @@
         loads[name] = copy
 
     pieces = [(ORDER[0], 0, part // 2), (ORDER[0], part // 2, part)] + [(q, 0, part) for q in ORDER[1:]]
+    load("nt", norm_train, nt)
+    load("ns", norm_step, ns)
     load("lq", low_query, lq)
     load("hq", high_query, hq)
     for n, (q, start, end) in enumerate(pieces):
@@ -149,8 +152,6 @@
             load("tv", train_value, tv)
             load("lv", low_value, lv)
             load("hv", high_value, hv)
-    load("nt", norm_train, nt)
-    load("ns", norm_step, ns)
 
     def merged(train, high, low):
         return train.astype(jnp.float32) + lax.dot_general(
@@ -174,22 +175,42 @@
 
     def only(core):
         return pl.when(me.core == LATE if core == LATE else me.core != LATE)
+
+    def fresh_copy():
+        return remote(fresh, ring.at[me.row], fresh_sem.at[0], fresh_sem.at[1], (0, me.col))
+
+    def make_fresh():
+        loads["nt"].wait()
+        loads["ns"].wait()
+        values = nt[...] + ns[...]
+        fresh[...] = jnp.concatenate([values, values], axis=1)
+
+    def send_fresh():
+        @pl.when(leader)
+        def _():
+            ring[me.row] = fresh[...]
+
+        @pl.when(jnp.logical_not(leader))
+        def _():
+            fresh_copy().start()
 
     loads["lq"].wait()
     loads["hq"].wait()
     for n, (q, start, end) in enumerate(pieces):
         cols = pl.ds(q * part + start, end - start)
         loads[n].wait()
+        if n == 1:
+            make_fresh()
         whole[me.row, q, start:end, :] = merged(tq[:, cols].T, hq[:, cols], lq[...]).astype(whole.dtype)
         if n == 0:
 
             @pl.when(leader)
             def _():
-                pl.semaphore_wait(barrier, len(peers) + len(steps))
+                pl.semaphore_wait(barrier, len(peers) + n_planes - 1)
 
             @pl.when(jnp.logical_not(leader))
             def _():
-                pl.semaphore_wait(barrier, len(peers))
+                pl.semaphore_wait(barrier, len(peers) + 1)
 
         if end == part:
             if n == 1:
@@ -209,98 +230,32 @@
                 send(link, 0, pl.ds(start, whole.shape[2] - start))
             else:
                 send(link, ORDER.index(q))
-
-    loads["nt"].wait()
-    loads["ns"].wait()
-    fresh = nt[...] + ns[...]
-    pair[me.core] = jnp.concatenate([fresh, fresh], axis=1)
-
-    def pair_copy(slot):
-        return remote(pair.at[slot], pair.at[slot], pair_sem.at[0], pair_sem.at[1], me.partner())
-
-    pair_copy(me.core).start()
-
-    def ring_copy(n, src, d):
-        return remote(src, src, ring_send, ring_recv.at[n], me.neighbour(d))
-
-    def column(dz):
-        return ring.at[pl.ds(((me.z + dz) % SIDE) * SIDE, SIDE)]
-
-    def line_copy(n):
-        return remote(lines, all_lines.at[me.x], line_sem.at[0], line_sem.at[1], me.along_x(n))
-
-    def norm_copy(link):
-        return remote(norm, norm, norm_send.at[link], norm_recv, me.neighbour(LINKS[link]))
-
-    passes = [((0, 0), (0, 1, 2, 3)), ((0, 1), (0, 2, 3)), ((0, 3), (2, 3)), ((0, 2), (2, 3))]
-    passes += [((1, y), (2,)) for y in range(SIDE)]
-
-    def pass_norm(places):
-        for (z, y), links in passes:
-            if (z, y) in places:
-
-                @pl.when((me.z == z) & (me.y == y))
-                def _():
-                    if (z, y) != (0, 0):
-                        norm_copy(0).wait_recv()
-                    for link in links:
-                        norm_copy(link).start()
-
-    def norm_step_of(step):
-        if step == 0:
-            pair_copy(1 - me.core).wait_recv()
-            lane = lax.broadcasted_iota(jnp.int32, (1, pair.shape[2]), 1)
-            ring[me.row] = jnp.where(lane < pair.shape[2] // CORES, pair[0], pair[1])
-        if step == 1:
-            ring_copy(0, ring.at[me.row], (0, 1)).start()
-            ring_copy(1, ring.at[me.row], (0, -1)).start()
-        if step == 2:
-            ring_copy(0, ring.at[me.at((0, -1))], (0, 1)).wait_recv()
-            ring_copy(1, ring.at[me.at((0, 1))], (0, -1)).wait_recv()
-            ring_copy(2, ring.at[me.at((0, -1))], (0, 1)).start()
-        if step == 3:
-            ring_copy(2, ring.at[me.at((0, -2))], (0, 1)).wait_recv()
-            ring_copy(3, column(0), (1, 0)).start()
-            ring_copy(4, column(0), (-1, 0)).start()
-        if step == 4:
-            ring_copy(3, column(-1), (1, 0)).wait_recv()
-            ring_copy(4, column(1), (-1, 0)).wait_recv()
-            ring_copy(5, column(-1), (1, 0)).start()
-        if step == 5:
-            ring_copy(5, column(-2), (1, 0)).wait_recv()
-
-            @pl.when(leader)
-            def _():
-                lines[...] = jnp.concatenate([ring[i] for i in range(blocks)], axis=0)
-                all_lines[me.x] = lines[...]
-                for n in steps:
-                    line_copy(n).start()
-
-        if step == 7:
-
-            @pl.when(leader)
-            def _():
-                three = all_lines.at[pl.ds(0, len(steps))]
-                every = remote(three, three, line_sem.at[0], line_sem.at[1], me.along_x(1))
-                every.wait_recv()
-                for x in range(SIDE):
-                    ordered[pl.Slice(x, blocks, SIDE), :] = all_lines[x]
-                norm[...] = ordered[...].astype(norm.dtype)
-
-            pass_norm([(0, 0)])
-        if step == 8:
-            pass_norm([(0, 1), (0, 3)])
-        if step == 9:
-            pass_norm([(0, 2)])
-        if step == 10:
-            pass_norm([(1, y) for y in range(SIDE)])
+        if n == 1:
+            send_fresh()
+
+    def norm_at_leader(group):
+        if group == 0:
+            some = ring.at[pl.ds(0, blocks - 1)]
+            remote(some, some, fresh_sem.at[0], fresh_sem.at[1], me.partner()).wait_recv()
+            lines[me.col] = jnp.concatenate([ring[i] for i in range(blocks)], axis=0)
+            for n in range(1, n_planes):
+                remote(lines.at[me.col], lines.at[me.col], line_sem.at[0], line_sem.at[1], me.plane(n)).start()
+        if group == 1:
+            some = lines.at[pl.ds(0, n_planes - 1)]
+            remote(some, some, line_sem.at[0], line_sem.at[1], me.partner()).wait()
+            lane = lax.broadcasted_iota(jnp.int32, lines.shape[1:], 1)
+            for x in range(SIDE):
+                both = jnp.where(lane < lines.shape[2] // CORES, lines[CORES * x], lines[CORES * x + 1])
+                ordered[pl.Slice(x, blocks, SIDE), :] = both
+            norm[...] = ordered[...].astype(norm.dtype)
+            for off in others:
+                remote(norm, norm, norm_sem.at[0], norm_sem.at[1], me.neighbour(off)).start()
 
     def send_slots(slots):
         for slot in slots:
             for link in range(len(LINKS)):
                 send(link, slot)
 
-    norm_steps = ((0, 1), (2, 3), (4, 5, 7), (8, 9, 10), ())
     for group, slots in enumerate(AFTER):
         arrive(group)
         if slots[0] < SPLIT:
@@ -311,13 +266,11 @@
             def _():
                 send_slots(slots)
 
-        for step in norm_steps[group]:
-            norm_step_of(step)
-        if 10 in norm_steps[group]:
-
-            @pl.when(me.z >= 2)
+        if group < 2:
+
+            @pl.when(leader)
             def _():
-                norm_copy(0).wait_recv()
+                norm_at_leader(group)
 
     arrive(5)
 
@@ -330,21 +283,15 @@
     def _():
         units(SPLIT, recv_sem.at[0]).wait_send()
 
-    pair_copy(me.core).wait_send()
-    around = ring.at[pl.ds(0, blocks - 1)]
-    remote(around, around, ring_send, ring_recv.at[0], me.partner()).wait_send()
-
     @pl.when(leader)
     def _():
-        three = all_lines.at[pl.ds(0, len(steps))]
-        remote(three, three, line_sem.at[0], line_sem.at[1], me.along_x(1)).wait_send()
-
-    for (z, y), links in passes:
-
-        @pl.when((me.z == z) & (me.y == y))
-        def _():
-            for link in links:
-                norm_copy(link).wait_send()
+        some = whole.at[0, 0, pl.ds(0, (blocks - 1) * (norm.shape[0] * norm.shape[1] // whole.shape[3]))]
+        remote(some, some, norm_sem.at[0], norm_sem.at[1], me.partner()).wait_send()
+
+    @pl.when(jnp.logical_not(leader))
+    def _():
+        fresh_copy().wait_send()
+        remote(norm, norm, norm_sem.at[0], norm_sem.at[1], me.partner()).wait_recv()
 
 
 def finish_kernel(whole, token, rest, send_sem, recv_sem):
@@ -475,20 +422,16 @@
             pltpu.VMEM((rank, tall), dtype),
             pltpu.VMEM((1, values), f32),
             pltpu.VMEM((1, values), f32),
-            pltpu.VMEM((CORES, 1, line), f32),
+            pltpu.VMEM((1, line), f32),
             pltpu.VMEM((n_rows, 1, line), f32),
-            pltpu.VMEM((n_rows, line), f32),
-            pltpu.VMEM((SIDE, n_rows, line), f32),
+            pltpu.VMEM((n_cols, n_rows, line), f32),
             pltpu.VMEM((SIDE * n_rows, line), f32),
             dma((15,)),
             dma(()),
             dma((len(GROUPS),)),
             dma((2,)),
-            dma(()),
-            dma((6,)),
             dma((2,)),
-            dma((len(LINKS),)),
-            dma(()),
+            dma((2,)),
         ],
         compiler_params=pltpu.CompilerParams(
             collective_id=0, has_side_effects=True, vmem_limit_bytes=24 * 2**20

time: 117 us -> 106 us (0.906)
  Pallas kernels: 115 us -> 105 us
    pallas_call x1, Pallas kernels: 89.8 us -> 83.7 us  [body(): pl.pallas_call(gather_kernel, out_shape=(shape((n_rows, QUARTERS, unit, d...]
    pallas_call x1, Pallas kernels: 18 us -> 14.2 us  [body(): pl.pallas_call(finish_kernel, out_shape=(shape((len(LINKS), SLOTS - SPLIT...]
where the time goes in v6:
time: 106 us
  Pallas kernels  105 us (99%)
    pallas_call x1, Pallas kernels, body(): pl.pallas_call(gather_kernel, out_shape=(shape((n_rows, QUARTERS, unit, d...  83.7 us
    pallas_call x1, Pallas kernels, body(): pl.pallas_call(finish_kernel, out_shape=(shape((len(LINKS), SLOTS - SPLIT...  14.2 us
    pallas_call x1, Pallas kernels, body(): pl.pallas_call(write_kernel, out_shape=(*outs, shape((8, 128), f32)), in_...  5.35 us

profile of v6, /device:TPU:1, one launch (start us, length us, event | category | flops | bytes accessed | tf_op | source)
XLA Modules:
  0.0 105.7 jit_solution(9362567795488036319)
XLA Ops:
  0.6 83.7 %gather.1 = (bf16[16,4,288,512]{3,2,1,0:T(8,128)(2,1)S(1)}, bf16[64,128]{1,0:T(8,128)(2,1)S(1)}) custom-call(bf16[512,1024]{1,0:T(8,128)(2,1)} %train_query.1, bf16[64,512]{1,0:T(8,128)(2,1)} %bitcast.8, bf16[64,1024]{1,0:T(8,128)(2,1)} %high_query.1, bf16[64,512]{1,0:T(8,128)(2,1)} %bitcast.9, bf16[64,512]{1,0:T(8,128)(2,1)} %bitcast.10, ...), custom_call_target="tpu_custom_call" | custom-call | tf_op jit(solution)/shard_map/gather/pallas_call | solution.py:405
  84.3 5.3 %write.1 = (bf16[1024,8192]{1,0:T(8,128)(2,1)}, bf16[64,8192]{1,0:T(8,128)(2,1)}, bf16[64,8192]{1,0:T(8,128)(2,1)}, f32[8,128]{1,0:T(8,128)S(1)}) custom-call(bf16[16,4,288,512]{3,2,1,0:T(8,128)(2,1)S(1)} %get-tuple-element.14.whole), custom_call_target="tpu_custom_call" | custom-call | tf_op jit(solution)/shard_map/write/pallas_call | solution.py:450
  89.7 14.2 %finish.1.rest = bf16[4,3,288,512]{3,2,1,0:T(8,128)(2,1)S(1)} custom-call(bf16[16,4,288,512]{3,2,1,0:T(8,128)(2,1)S(1)} %get-tuple-element.14.whole, f32[8,128]{1,0:T(8,128)S(1)} %get-tuple-element.15.token), custom_call_target="tpu_custom_call" | custom-call | tf_op jit(solution)/shard_map/finish/pallas_call | solution.py:459
  103.8 1.8 %write_rest.1 = (bf16[1024,8192]{1,0:T(8,128)(2,1)}, bf16[64,8192]{1,0:T(8,128)(2,1)}, bf16[64,8192]{1,0:T(8,128)(2,1)}, bf16[64,128]{1,0:T(8,128)(2,1)}) custom-call(bf16[16,4,288,512]{3,2,1,0:T(8,128)(2,1)S(1)} %get-tuple-element.14.whole, bf16[4,3,288,512]{3,2,1,0:T(8,128)(2,1)S(1)} %finish.1.rest, ...), custom_call_target="tpu_custom_call", output_to_operand_aliasing={{0}: (3, {}), {1}: (4, {}), {2}: (5, {})} | custom-call | tf_op jit(solution)/shard_map/write_rest/pallas_call | solution.py:470

commit v7 on v6

--- a/solution.py
+++ b/solution.py
@@ -111,23 +111,30 @@
     norm_train, norm_step,
     whole, norm,
     tq, lq, hq, tk, lk, hk, tv, lv, hv, nt, ns, fresh, ring, lines, ordered,
-    load_sem, send_sem, recv_sem, fresh_sem, line_sem, norm_sem,
+    load_sem, send_sem, recv_sem, fresh_sem, column_sem, line_sem, norm_sem,
 ):
     me = Place()
     wide = tq.shape[1]
     part = wide // QUARTERS
     blocks = whole.shape[0]
-    leader = (me.z == 0) & (me.y == 0)
+    top = me.z == 0
+    leader = top & (me.y == 0)
+    head = top & (me.y != 0)
     n_planes = lines.shape[0]
-    others = [(dz, dy) for dz in range(SIDE) for dy in range(SIDE) if (dz, dy) != (0, 0)]
+    column = [(dz, 0) for dz in range(1, SIDE)]
+    heads = [(0, dy) for dy in range(1, SIDE)]
 
     barrier = pltpu.get_barrier_semaphore()
     peers = [me.neighbour(d) for d in LINKS] + [me.partner()]
     signal_all(barrier, peers)
 
+    @pl.when(top)
+    def _():
+        signal_all(barrier, [me.neighbour((2, 0))])
+
     @pl.when(leader)
     def _():
-        signal_all(barrier, [me.neighbour(off) for off in others] + [me.plane(n) for n in range(1, n_planes)])
+        signal_all(barrier, [me.neighbour((0, 2))] + [me.plane(n) for n in range(1, n_planes)])
 
     loads = {}
 
@@ -177,7 +184,22 @@
         return pl.when(me.core == LATE if core == LATE else me.core != LATE)
 
     def fresh_copy():
-        return remote(fresh, ring.at[me.row], fresh_sem.at[0], fresh_sem.at[1], (0, me.col))
+        return remote(fresh, ring.at[me.y * SIDE + me.z], fresh_sem.at[0], fresh_sem.at[1], (me.y, me.col))
+
+    def column_copy():
+        part_of_ring = ring.at[pl.ds(me.y * SIDE, SIDE)]
+        return remote(part_of_ring, part_of_ring, column_sem.at[0], column_sem.at[1], (0, me.col))
+
+    def ring_lines(count, sem):
+        some = ring.at[pl.ds(0, count)]
+        return remote(some, some, sem.at[0], sem.at[1], me.partner())
+
+    def norm_copy(off):
+        return remote(norm, norm, norm_sem.at[0], norm_sem.at[1], me.neighbour(off))
+
+    def norm_sent(count):
+        some = whole.at[0, 0, pl.ds(0, count * norm.shape[0] * norm.shape[1] // whole.shape[3])]
+        remote(some, some, norm_sem.at[0], norm_sem.at[1], me.partner()).wait_send()
 
     def make_fresh():
         loads["nt"].wait()
@@ -186,11 +208,11 @@
         fresh[...] = jnp.concatenate([values, values], axis=1)
 
     def send_fresh():
-        @pl.when(leader)
+        @pl.when(top)
         def _():
-            ring[me.row] = fresh[...]
-
-        @pl.when(jnp.logical_not(leader))
+            ring[me.y * SIDE + me.z] = fresh[...]
+
+        @pl.when(jnp.logical_not(top))
         def _():
             fresh_copy().start()
 
@@ -208,9 +230,15 @@
             def _():
                 pl.semaphore_wait(barrier, len(peers) + n_planes - 1)
 
-            @pl.when(jnp.logical_not(leader))
+            far = (me.z == 2) | (top & (me.y == 2))
+
+            @pl.when(far)
             def _():
                 pl.semaphore_wait(barrier, len(peers) + 1)
+
+            @pl.when(jnp.logical_not(leader | far))
+            def _():
+                pl.semaphore_wait(barrier, len(peers))
 
         if end == part:
             if n == 1:
@@ -233,23 +261,43 @@
         if n == 1:
             send_fresh()
 
-    def norm_at_leader(group):
+    def norm_on_its_way(group):
         if group == 0:
-            some = ring.at[pl.ds(0, blocks - 1)]
-            remote(some, some, fresh_sem.at[0], fresh_sem.at[1], me.partner()).wait_recv()
-            lines[me.col] = jnp.concatenate([ring[i] for i in range(blocks)], axis=0)
-            for n in range(1, n_planes):
-                remote(lines.at[me.col], lines.at[me.col], line_sem.at[0], line_sem.at[1], me.plane(n)).start()
+
+            @pl.when(top)
+            def _():
+                ring_lines(len(column), fresh_sem).wait_recv()
+
+            @pl.when(head)
+            def _():
+                column_copy().start()
+
         if group == 1:
-            some = lines.at[pl.ds(0, n_planes - 1)]
-            remote(some, some, line_sem.at[0], line_sem.at[1], me.partner()).wait()
-            lane = lax.broadcasted_iota(jnp.int32, lines.shape[1:], 1)
-            for x in range(SIDE):
-                both = jnp.where(lane < lines.shape[2] // CORES, lines[CORES * x], lines[CORES * x + 1])
-                ordered[pl.Slice(x, blocks, SIDE), :] = both
-            norm[...] = ordered[...].astype(norm.dtype)
-            for off in others:
-                remote(norm, norm, norm_sem.at[0], norm_sem.at[1], me.neighbour(off)).start()
+
+            @pl.when(leader)
+            def _():
+                ring_lines(len(heads) * SIDE, column_sem).wait_recv()
+                in_order = [ring[(i % SIDE) * SIDE + i // SIDE] for i in range(blocks)]
+                lines[me.col] = jnp.concatenate(in_order, axis=0)
+                for n in range(1, n_planes):
+                    remote(lines.at[me.col], lines.at[me.col], line_sem.at[0], line_sem.at[1], me.plane(n)).start()
+                some = lines.at[pl.ds(0, n_planes - 1)]
+                remote(some, some, line_sem.at[0], line_sem.at[1], me.partner()).wait()
+                lane = lax.broadcasted_iota(jnp.int32, lines.shape[1:], 1)
+                for x in range(SIDE):
+                    both = jnp.where(lane < lines.shape[2] // CORES, lines[CORES * x], lines[CORES * x + 1])
+                    ordered[pl.Slice(x, blocks, SIDE), :] = both
+                norm[...] = ordered[...].astype(norm.dtype)
+                for off in heads + column:
+                    norm_copy(off).start()
+
+        if group == 2:
+
+            @pl.when(head)
+            def _():
+                norm_copy((1, 0)).wait_recv()
+                for off in column:
+                    norm_copy(off).start()
 
     def send_slots(slots):
         for slot in slots:
@@ -258,6 +306,7 @@
 
     for group, slots in enumerate(AFTER):
         arrive(group)
+        norm_on_its_way(group)
         if slots[0] < SPLIT:
             send_slots(slots)
         else:
@@ -266,12 +315,6 @@
             def _():
                 send_slots(slots)
 
-        if group < 2:
-
-            @pl.when(leader)
-            def _():
-                norm_at_leader(group)
-
     arrive(5)
 
     @only(1 - LATE)
@@ -285,13 +328,17 @@
 
     @pl.when(leader)
     def _():
-        some = whole.at[0, 0, pl.ds(0, (blocks - 1) * (norm.shape[0] * norm.shape[1] // whole.shape[3]))]
-        remote(some, some, norm_sem.at[0], norm_sem.at[1], me.partner()).wait_send()
-
-    @pl.when(jnp.logical_not(leader))
+        norm_sent(len(heads) + len(column))
+
+    @pl.when(head)
+    def _():
+        column_copy().wait_send()
+        norm_sent(len(column))
+
+    @pl.when(jnp.logical_not(top))
     def _():
         fresh_copy().wait_send()
-        remote(norm, norm, norm_sem.at[0], norm_sem.at[1], me.partner()).wait_recv()
+        norm_copy((1, 0)).wait_recv()
 
 
 def finish_kernel(whole, token, rest, send_sem, recv_sem):
@@ -429,6 +476,7 @@
             dma((15,)),
             dma(()),
             dma((len(GROUPS),)),
+            dma((2,)),
             dma((2,)),
             dma((2,)),
             dma((2,)),

time: 106 us -> 106 us (level)
  no operation moved by 1% of the time
where the time goes in v7:
time: 106 us
  Pallas kernels  105 us (99%)
    pallas_call x1, Pallas kernels, body(): pl.pallas_call(gather_kernel, out_shape=(shape((n_rows, QUARTERS, unit, d...  83.7 us
    pallas_call x1, Pallas kernels, body(): pl.pallas_call(finish_kernel, out_shape=(shape((len(LINKS), SLOTS - SPLIT...  14.2 us
    pallas_call x1, Pallas kernels, body(): pl.pallas_call(write_kernel, out_shape=(*outs, shape((8, 128), f32)), in_...  5.35 us

profile of v7, /device:TPU:1, one launch (start us, length us, event | category | flops | bytes accessed | tf_op | source)
XLA Modules:
  0.0 105.7 jit_solution(3541308673124104815)
XLA Ops:
  0.6 83.7 %gather.1 = (bf16[16,4,288,512]{3,2,1,0:T(8,128)(2,1)S(1)}, bf16[64,128]{1,0:T(8,128)(2,1)S(1)}) custom-call(bf16[512,1024]{1,0:T(8,128)(2,1)} %train_query.1, bf16[64,512]{1,0:T(8,128)(2,1)} %bitcast.8, bf16[64,1024]{1,0:T(8,128)(2,1)} %high_query.1, bf16[64,512]{1,0:T(8,128)(2,1)} %bitcast.9, bf16[64,512]{1,0:T(8,128)(2,1)} %bitcast.10, ...), custom_call_target="tpu_custom_call" | custom-call | tf_op jit(solution)/shard_map/gather/pallas_call | solution.py:452
  84.3 5.3 %write.1 = (bf16[1024,8192]{1,0:T(8,128)(2,1)}, bf16[64,8192]{1,0:T(8,128)(2,1)}, bf16[64,8192]{1,0:T(8,128)(2,1)}, f32[8,128]{1,0:T(8,128)S(1)}) custom-call(bf16[16,4,288,512]{3,2,1,0:T(8,128)(2,1)S(1)} %get-tuple-element.14.whole), custom_call_target="tpu_custom_call" | custom-call | tf_op jit(solution)/shard_map/write/pallas_call | solution.py:498
  89.7 14.2 %finish.1.rest = bf16[4,3,288,512]{3,2,1,0:T(8,128)(2,1)S(1)} custom-call(bf16[16,4,288,512]{3,2,1,0:T(8,128)(2,1)S(1)} %get-tuple-element.14.whole, f32[8,128]{1,0:T(8,128)S(1)} %get-tuple-element.15.token), custom_call_target="tpu_custom_call" | custom-call | tf_op jit(solution)/shard_map/finish/pallas_call | solution.py:507
  103.9 1.8 %write_rest.1 = (bf16[1024,8192]{1,0:T(8,128)(2,1)}, bf16[64,8192]{1,0:T(8,128)(2,1)}, bf16[64,8192]{1,0:T(8,128)(2,1)}, bf16[64,128]{1,0:T(8,128)(2,1)}) custom-call(bf16[16,4,288,512]{3,2,1,0:T(8,128)(2,1)S(1)} %get-tuple-element.14.whole, bf16[4,3,288,512]{3,2,1,0:T(8,128)(2,1)S(1)} %finish.1.rest, ...), custom_call_target="tpu_custom_call", output_to_operand_aliasing={{0}: (3, {}), {1}: (4, {}), {2}: (5, {})} | custom-call | tf_op jit(solution)/shard_map/write_rest/pallas_call | solution.py:518

commit v8 on v7

--- a/solution.py
+++ b/solution.py
@@ -13,6 +13,7 @@
 LINKS = ((0, 1), (0, -1), (1, 0), (-1, 0))
 LATE = 1
 SPLIT = 12
+LEAD = 2
 ORDER = (0, 2, 1, 3)
 
 
@@ -118,23 +119,25 @@
     part = wide // QUARTERS
     blocks = whole.shape[0]
     top = me.z == 0
-    leader = top & (me.y == 0)
-    head = top & (me.y != 0)
+    leader = top & (me.y == LEAD)
+    head = top & (me.y != LEAD)
     n_planes = lines.shape[0]
     column = [(dz, 0) for dz in range(1, SIDE)]
     heads = [(0, dy) for dy in range(1, SIDE)]
 
     barrier = pltpu.get_barrier_semaphore()
     peers = [me.neighbour(d) for d in LINKS] + [me.partner()]
-    signal_all(barrier, peers)
-
-    @pl.when(top)
-    def _():
-        signal_all(barrier, [me.neighbour((2, 0))])
-
-    @pl.when(leader)
-    def _():
-        signal_all(barrier, [me.neighbour((0, 2))] + [me.plane(n) for n in range(1, n_planes)])
+
+    def greet():
+        signal_all(barrier, peers)
+
+        @pl.when(top)
+        def _():
+            signal_all(barrier, [me.neighbour((2, 0))])
+
+        @pl.when(leader)
+        def _():
+            signal_all(barrier, [me.neighbour((0, 2))] + [me.plane(n) for n in range(1, n_planes)])
 
     loads = {}
 
@@ -144,13 +147,15 @@
         loads[name] = copy
 
     pieces = [(ORDER[0], 0, part // 2), (ORDER[0], part // 2, part)] + [(q, 0, part) for q in ORDER[1:]]
-    load("nt", norm_train, nt)
-    load("ns", norm_step, ns)
     load("lq", low_query, lq)
     load("hq", high_query, hq)
     for n, (q, start, end) in enumerate(pieces):
         cols = pl.ds(q * part + start, end - start)
         load(n, train_query.at[:, cols], tq.at[:, cols])
+        if n == 0:
+            greet()
+            load("nt", norm_train, nt)
+            load("ns", norm_step, ns)
         if n == 1:
             load("tk", train_key, tk)
             load("lk", low_key, lk)
@@ -188,7 +193,7 @@
 
     def column_copy():
         part_of_ring = ring.at[pl.ds(me.y * SIDE, SIDE)]
-        return remote(part_of_ring, part_of_ring, column_sem.at[0], column_sem.at[1], (0, me.col))
+        return remote(part_of_ring, part_of_ring, column_sem.at[0], column_sem.at[1], (LEAD, me.col))
 
     def ring_lines(count, sem):
         some = ring.at[pl.ds(0, count)]
@@ -230,7 +235,7 @@
             def _():
                 pl.semaphore_wait(barrier, len(peers) + n_planes - 1)
 
-            far = (me.z == 2) | (top & (me.y == 2))
+            far = (me.z == 2) | (top & (me.y == (LEAD + 2) % SIDE))
 
             @pl.when(far)
             def _():

time: 106 us -> 106 us (level)
  no operation moved by 1% of the time
where the time goes in v8:
time: 106 us
  Pallas kernels  105 us (99%)
    pallas_call x1, Pallas kernels, body(): pl.pallas_call(gather_kernel, out_shape=(shape((n_rows, QUARTERS, unit, d...  83.9 us
    pallas_call x1, Pallas kernels, body(): pl.pallas_call(finish_kernel, out_shape=(shape((len(LINKS), SLOTS - SPLIT...  14.2 us
    pallas_call x1, Pallas kernels, body(): pl.pallas_call(write_kernel, out_shape=(*outs, shape((8, 128), f32)), in_...  5.35 us

profile of v8, /device:TPU:1, one launch (start us, length us, event | category | flops | bytes accessed | tf_op | source)
XLA Modules:
  0.0 106.0 jit_solution(10001330761969353616)
XLA Ops:
  0.6 83.9 %gather.1 = (bf16[16,4,288,512]{3,2,1,0:T(8,128)(2,1)S(1)}, bf16[64,128]{1,0:T(8,128)(2,1)S(1)}) custom-call(bf16[512,1024]{1,0:T(8,128)(2,1)} %train_query.1, bf16[64,512]{1,0:T(8,128)(2,1)} %bitcast.8, bf16[64,1024]{1,0:T(8,128)(2,1)} %high_query.1, bf16[64,512]{1,0:T(8,128)(2,1)} %bitcast.9, bf16[64,512]{1,0:T(8,128)(2,1)} %bitcast.10, ...), custom_call_target="tpu_custom_call" | custom-call | tf_op jit(solution)/shard_map/gather/pallas_call | solution.py:457
  84.6 5.3 %write.1 = (bf16[1024,8192]{1,0:T(8,128)(2,1)}, bf16[64,8192]{1,0:T(8,128)(2,1)}, bf16[64,8192]{1,0:T(8,128)(2,1)}, f32[8,128]{1,0:T(8,128)S(1)}) custom-call(bf16[16,4,288,512]{3,2,1,0:T(8,128)(2,1)S(1)} %get-tuple-element.14.whole), custom_call_target="tpu_custom_call" | custom-call | tf_op jit(solution)/shard_map/write/pallas_call | solution.py:503
  89.9 14.2 %finish.1.rest = bf16[4,3,288,512]{3,2,1,0:T(8,128)(2,1)S(1)} custom-call(bf16[16,4,288,512]{3,2,1,0:T(8,128)(2,1)S(1)} %get-tuple-element.14.whole, f32[8,128]{1,0:T(8,128)S(1)} %get-tuple-element.15.token), custom_call_target="tpu_custom_call" | custom-call | tf_op jit(solution)/shard_map/finish/pallas_call | solution.py:512
  104.1 1.8 %write_rest.1 = (bf16[1024,8192]{1,0:T(8,128)(2,1)}, bf16[64,8192]{1,0:T(8,128)(2,1)}, bf16[64,8192]{1,0:T(8,128)(2,1)}, bf16[64,128]{1,0:T(8,128)(2,1)}) custom-call(bf16[16,4,288,512]{3,2,1,0:T(8,128)(2,1)S(1)} %get-tuple-element.14.whole, bf16[4,3,288,512]{3,2,1,0:T(8,128)(2,1)S(1)} %finish.1.rest, ...), custom_call_target="tpu_custom_call", output_to_operand_aliasing={{0}: (3, {}), {1}: (4, {}), {2}: (5, {})} | custom-call | tf_op jit(solution)/shard_map/write_rest/pallas_call | solution.py:523

commit v9 on v8

--- a/solution.py
+++ b/solution.py
@@ -13,6 +13,7 @@
 LINKS = ((0, 1), (0, -1), (1, 0), (-1, 0))
 LATE = 1
 SPLIT = 12
+CUT = 128
 LEAD = 2
 ORDER = (0, 2, 1, 3)
 
@@ -65,9 +66,11 @@
 ARRIVES = {arriving(*unit): unit for unit in UNITS}
 assert len(ARRIVES) == len(UNITS) == (SIDE * SIDE - 1) * QUARTERS
 LAST = [unit for unit in UNITS if unit[1] >= SPLIT]
-GROUPS = ((0, 1), (2, 3), (6,), (4, 5, 7, 8), (10, 11), (9,), (12, 13, 14))
+FINAL = SLOTS - 1
+assert all(arriving(link, FINAL)[0] == (2, 2) for link in range(len(LINKS)))
+GROUPS = ((0, 1), (2, 3), (6,), (4, 5, 7, 8), (10, 11), (9,), (12, 13), (14,))
 GROUP_OF = {slot: group for group, slots in enumerate(GROUPS) for slot in slots}
-assert sorted(GROUP_OF) == list(range(SLOTS)) and GROUPS[-1] == tuple(range(SPLIT, SLOTS))
+assert sorted(GROUP_OF) == list(range(SLOTS)) and GROUPS[-2] + GROUPS[-1] == tuple(range(SPLIT, SLOTS))
 AFTER = ((4, 5), (6, 7, 8, 9), (10, 11), (12, 13), (14,))
 for _group, _slots in enumerate(AFTER):
     for _slot in _slots:
@@ -112,7 +115,7 @@
     norm_train, norm_step,
     whole, norm,
     tq, lq, hq, tk, lk, hk, tv, lv, hv, nt, ns, fresh, ring, lines, ordered,
-    load_sem, send_sem, recv_sem, fresh_sem, column_sem, line_sem, norm_sem,
+    load_sem, send_sem, cut_sem, recv_sem, fresh_sem, column_sem, line_sem, norm_sem,
 ):
     me = Place()
     wide = tq.shape[1]
@@ -173,7 +176,8 @@
     def unit_copy(link, slot, what, rows=slice(None)):
         off, q = what
         unit = whole.at[me.at(off), q, rows]
-        return remote(unit, unit, send_sem, recv_sem.at[GROUP_OF[slot]], me.neighbour(LINKS[link]))
+        sem = cut_sem if slot == FINAL else send_sem
+        return remote(unit, unit, sem, recv_sem.at[GROUP_OF[slot]], me.neighbour(LINKS[link]))
 
     def send(link, slot, rows=slice(None)):
         unit_copy(link, slot, SENDS[link][slot], rows).start()
@@ -307,7 +311,7 @@
     def send_slots(slots):
         for slot in slots:
             for link in range(len(LINKS)):
-                send(link, slot)
+                send(link, slot, pl.ds(0, CUT) if slot == FINAL else slice(None))
 
     for group, slots in enumerate(AFTER):
         arrive(group)
@@ -325,7 +329,9 @@
     @only(1 - LATE)
     def _():
         arrive(6)
-        units(SLOTS, recv_sem.at[0]).wait_send()
+        cut = whole.at[pl.ds(0, len(LINKS)), 0, pl.ds(0, CUT)]
+        remote(cut, cut, cut_sem, recv_sem.at[7], me.partner()).wait()
+        units(FINAL, recv_sem.at[0]).wait_send()
 
     @only(LATE)
     def _():
@@ -349,45 +355,63 @@
 def finish_kernel(whole, token, rest, send_sem, recv_sem):
     del token
     me = Place()
+    barrier = pltpu.get_barrier_semaphore()
+    signal_all(barrier, [me.neighbour(d) for d in LINKS])
+    pl.semaphore_wait(barrier, len(LINKS))
+
+    def send(link, slot, rows):
+        off, q = SENDS[link][slot]
+        source, target = whole.at[me.at(off), q, rows], rest.at[link, slot - SPLIT, rows]
+        remote(source, target, send_sem, recv_sem, me.neighbour(LINKS[link])).start()
 
     @pl.when(me.core == LATE)
     def _():
-        barrier = pltpu.get_barrier_semaphore()
-        signal_all(barrier, [me.neighbour(d) for d in LINKS])
-        pl.semaphore_wait(barrier, len(LINKS))
         for link, slot in LAST:
-            off, q = SENDS[link][slot]
-            unit = whole.at[me.at(off), q]
-            remote(unit, rest.at[link, slot - SPLIT], send_sem, recv_sem, me.neighbour(LINKS[link])).start()
+            send(link, slot, slice(None))
         remote(rest, rest, send_sem, recv_sem, me.partner()).wait()
 
-
-def write_unit(source, block, quarter, outs, sems):
+    @pl.when(me.core != LATE)
+    def _():
+        left = whole.shape[2] - CUT
+        for link in range(len(LINKS)):
+            send(link, FINAL, pl.ds(CUT, left))
+        cut = rest.at[pl.ds(0, len(LINKS)), 0, pl.ds(0, left)]
+        remote(cut, cut, send_sem, recv_sem, me.partner()).wait()
+
+
+def write_rows(source, block, quarter, outs, sems, start, end):
     out_query, out_key, out_value = outs
     rows, depth = source.shape
     part = out_query.shape[0] // QUARTERS
     half = rows - part
     at = pl.ds(pl.multiple_of(block * depth, depth), depth)
-    small = (out_key if quarter < 2 else out_value).at[pl.ds((quarter % 2) * half, half), at]
-    pltpu.make_async_copy(source.at[pl.ds(0, part)], out_query.at[pl.ds(quarter * part, part), at], sems[0]).start()
-    pltpu.make_async_copy(source.at[pl.ds(part, half)], small, sems[1 + quarter // 2]).start()
-
-
-def wait_units(count, unit_bytes, out, sem):
-    rows = count * unit_bytes // (out.shape[1] * out.dtype.itemsize)
-    same = out.at[pl.ds(0, rows)]
+    if end <= part:
+        target, sem = out_query.at[pl.ds(quarter * part + start, end - start), at], sems[0]
+    else:
+        assert (start, end) == (part, rows)
+        target, sem = (out_key if quarter < 2 else out_value).at[pl.ds((quarter % 2) * half, half), at], sems[1]
+    pltpu.make_async_copy(source.at[pl.ds(start, end - start)], target, sem).start()
+
+
+def write_unit(source, block, quarter, outs, sems):
+    part = outs[0].shape[0] // QUARTERS
+    write_rows(source, block, quarter, outs, sems, 0, part)
+    write_rows(source, block, quarter, outs, sems, part, source.shape[0])
+
+
+def wait_rows(count, whole, out, sem):
+    same = out.at[pl.ds(0, count * whole.shape[-1] // out.shape[1])]
     pltpu.make_async_copy(same, same, sem).wait()
-
-
-def unit_bytes_of(whole):
-    return whole.shape[-2] * whole.shape[-1] * whole.dtype.itemsize
 
 
 def write_kernel(whole, out_query, out_key, out_value, token, sem):
     me = Place()
     outs = (out_query, out_key, out_value)
+    blocks, _, rows, _ = whole.shape
+    part = out_query.shape[0] // QUARTERS
     token[...] = jnp.zeros_like(token)
     late = {arriving(*unit) for unit in LAST}
+    first, second = sem.at[0], sem.at[1]
 
     @pl.when(me.core == LATE)
     def _():
@@ -397,8 +421,23 @@
                 if (off, q) not in late:
                     count += 1
                     block = me.at(off)
-                    write_unit(whole.at[block, q], block, q, outs, (sem, sem, sem))
-        wait_units(count, unit_bytes_of(whole), out_query, sem)
+                    write_unit(whole.at[block, q], block, q, outs, (first, first))
+        wait_rows(count * rows, whole, out_query, first)
+
+    @pl.when(me.core != LATE)
+    def _():
+        final = me.at((2, 2))
+
+        @pl.loop(1, blocks)
+        def _(n):
+            block = (final + n) % blocks
+            for q in range(QUARTERS):
+                write_unit(whole.at[block, q], block, q, outs, (first, second))
+
+        for q in range(QUARTERS):
+            write_rows(whole.at[final, q], final, q, outs, (first, second), 0, CUT)
+        wait_rows(QUARTERS * ((blocks - 1) * part + CUT), whole, out_query, first)
+        wait_rows(QUARTERS * (blocks - 1) * (rows - part), whole, out_query, second)
 
 
 def write_rest_kernel(
@@ -407,26 +446,26 @@
     del in_query, in_key, in_value
     me = Place()
     outs = (out_query, out_key, out_value)
+    rows = whole.shape[2]
+    part = out_query.shape[0] // QUARTERS
     norm_copy = pltpu.make_async_copy(norm, out_norm, norm_sem)
     norm_copy.start()
 
     @pl.when(me.core == LATE)
     def _():
-        first = sem.at[0]
         for link, slot in LAST:
             off, q = arriving(link, slot)
-            write_unit(rest.at[link, slot - SPLIT], me.at(off), q, outs, (first, first, first))
-        wait_units(len(LAST), unit_bytes_of(whole), out_query, first)
+            write_unit(rest.at[link, slot - SPLIT], me.at(off), q, outs, (sem, sem))
+        wait_rows(len(LAST) * rows, whole, out_query, sem)
 
     @pl.when(me.core != LATE)
     def _():
-        @pl.loop(0, whole.shape[0])
-        def _(block):
-            for q in range(QUARTERS):
-                write_unit(whole.at[block, q], block, q, outs, [sem.at[n] for n in range(len(outs))])
-
-        for n, out in enumerate(outs):
-            pltpu.make_async_copy(out, out, sem.at[n]).wait()
+        for link in range(len(LINKS)):
+            off, q = arriving(link, FINAL)
+            source = rest.at[link, FINAL - SPLIT]
+            write_rows(source, me.at(off), q, outs, (sem, sem), CUT, part)
+            write_rows(source, me.at(off), q, outs, (sem, sem), part, rows)
+        wait_rows(len(LINKS) * (rows - CUT), whole, out_query, sem)
 
     norm_copy.wait()
 
@@ -480,6 +519,7 @@
             pltpu.VMEM((SIDE * n_rows, line), f32),
             dma((15,)),
             dma(()),
+            dma(()),
             dma((len(GROUPS),)),
             dma((2,)),
             dma((2,)),
@@ -505,7 +545,7 @@
         out_shape=(*outs, shape((8, 128), f32)),
         in_specs=[vmem],
         out_specs=[anywhere] * 3 + [vmem],
-        scratch_shapes=[dma(())],
+        scratch_shapes=[dma((2,))],
         compiler_params=pltpu.CompilerParams(vmem_limit_bytes=4 * 2**20),
         name="write",
     )(*pin(pltpu.VMEM, whole))
@@ -526,7 +566,7 @@
         in_specs=[vmem] * 3 + [anywhere] * 3,
         out_specs=[anywhere] * 4,
         input_output_aliases={3: 0, 4: 1, 5: 2},
-        scratch_shapes=[dma((len(outs),)), dma(())],
+        scratch_shapes=[dma(()), dma(())],
         compiler_params=pltpu.CompilerParams(vmem_limit_bytes=4 * 2**20),
         name="write_rest",
     )(*pin(pltpu.VMEM, whole, rest, norm), *pin(pltpu.HBM, out_query, out_key, out_value))

time: 106 us -> 106 us (level)
  no operation moved by 1% of the time
where the time goes in v9:
time: 106 us; the launch traced here: 105 us
  Pallas kernels  104 us (98%)
    pallas_call x1, Pallas kernels, body(): pl.pallas_call(gather_kernel, out_shape=(shape((n_rows, QUARTERS, unit, d...  84 us
    pallas_call x1, Pallas kernels, body(): pl.pallas_call(finish_kernel, out_shape=(shape((len(LINKS), SLOTS - SPLIT...  13.2 us
    pallas_call x1, Pallas kernels, body(): pl.pallas_call(write_kernel, out_shape=(*outs, shape((8, 128), f32)), in_...  5.36 us

profile of v9, /device:TPU:1, one launch (start us, length us, event | category | flops | bytes accessed | tf_op | source)
XLA Modules:
  0.0 105.0 jit_solution(2110445598312124980)
XLA Ops:
  0.6 84.0 %gather.1 = (bf16[16,4,288,512]{3,2,1,0:T(8,128)(2,1)S(1)}, bf16[64,128]{1,0:T(8,128)(2,1)S(1)}) custom-call(bf16[512,1024]{1,0:T(8,128)(2,1)} %train_query.1, bf16[64,512]{1,0:T(8,128)(2,1)} %bitcast.8, bf16[64,1024]{1,0:T(8,128)(2,1)} %high_query.1, bf16[64,512]{1,0:T(8,128)(2,1)} %bitcast.9, bf16[64,512]{1,0:T(8,128)(2,1)} %bitcast.10, ...), custom_call_target="tpu_custom_call" | custom-call | tf_op jit(solution)/shard_map/gather/pallas_call | solution.py:496
  84.6 5.4 %write.1 = (bf16[1024,8192]{1,0:T(8,128)(2,1)}, bf16[64,8192]{1,0:T(8,128)(2,1)}, bf16[64,8192]{1,0:T(8,128)(2,1)}, f32[8,128]{1,0:T(8,128)S(1)}) custom-call(bf16[16,4,288,512]{3,2,1,0:T(8,128)(2,1)S(1)} %get-tuple-element.14.whole), custom_call_target="tpu_custom_call" | custom-call | tf_op jit(solution)/shard_map/write/pallas_call | solution.py:543
  90.0 13.2 %finish.1.rest = bf16[4,3,288,512]{3,2,1,0:T(8,128)(2,1)S(1)} custom-call(bf16[16,4,288,512]{3,2,1,0:T(8,128)(2,1)S(1)} %get-tuple-element.14.whole, f32[8,128]{1,0:T(8,128)S(1)} %get-tuple-element.15.token), custom_call_target="tpu_custom_call" | custom-call | tf_op jit(solution)/shard_map/finish/pallas_call | solution.py:552
  103.2 1.8 %write_rest.1 = (bf16[1024,8192]{1,0:T(8,128)(2,1)}, bf16[64,8192]{1,0:T(8,128)(2,1)}, bf16[64,8192]{1,0:T(8,128)(2,1)}, bf16[64,128]{1,0:T(8,128)(2,1)}) custom-call(bf16[16,4,288,512]{3,2,1,0:T(8,128)(2,1)S(1)} %get-tuple-element.14.whole, bf16[4,3,288,512]{3,2,1,0:T(8,128)(2,1)S(1)} %finish.1.rest, ...), custom_call_target="tpu_custom_call", output_to_operand_aliasing={{0}: (3, {}), {1}: (4, {}), {2}: (5, {})} | custom-call | tf_op jit(solution)/shard_map/write_rest/pallas_call | solution.py:563

commit v10 on v8

--- a/solution.py
+++ b/solution.py
@@ -12,7 +12,8 @@
 CORES = 2
 LINKS = ((0, 1), (0, -1), (1, 0), (-1, 0))
 LATE = 1
-SPLIT = 12
+SPLIT = 13
+HEAD_START = 2900
 LEAD = 2
 ORDER = (0, 2, 1, 3)
 
@@ -65,11 +66,12 @@
 ARRIVES = {arriving(*unit): unit for unit in UNITS}
 assert len(ARRIVES) == len(UNITS) == (SIDE * SIDE - 1) * QUARTERS
 LAST = [unit for unit in UNITS if unit[1] >= SPLIT]
-GROUPS = ((0, 1), (2, 3), (6,), (4, 5, 7, 8), (10, 11), (9,), (12, 13, 14))
+GROUPS = ((0, 1), (2, 3), (6,), (4, 5, 7, 8), (10, 11), (9, 12), (13, 14))
 GROUP_OF = {slot: group for group, slots in enumerate(GROUPS) for slot in slots}
 assert sorted(GROUP_OF) == list(range(SLOTS)) and GROUPS[-1] == tuple(range(SPLIT, SLOTS))
-AFTER = ((4, 5), (6, 7, 8, 9), (10, 11), (12, 13), (14,))
-for _group, _slots in enumerate(AFTER):
+AFTER = ((4, 5), (6, 7, 8, 9), (10, 11), (12,), (13,), (14,))
+NEEDS = (0, 1, 2, 3, 3, 4)
+for _group, _slots in zip(NEEDS, AFTER, strict=True):
     for _slot in _slots:
         for _link in range(len(LINKS)):
             assert GROUP_OF[ARRIVES[SENDS[_link][_slot]][1]] <= _group
@@ -244,6 +246,10 @@
             @pl.when(jnp.logical_not(leader | far))
             def _():
                 pl.semaphore_wait(barrier, len(peers))
+
+            @only(1 - LATE)
+            def _():
+                pl.delay(HEAD_START)
 
         if end == part:
             if n == 1:
@@ -309,9 +315,12 @@
             for link in range(len(LINKS)):
                 send(link, slot)
 
-    for group, slots in enumerate(AFTER):
-        arrive(group)
-        norm_on_its_way(group)
+    waited = -1
+    for group, slots in zip(NEEDS, AFTER, strict=True):
+        if group != waited:
+            waited = group
+            arrive(group)
+            norm_on_its_way(group)
         if slots[0] < SPLIT:
             send_slots(slots)
         else:

time: 106 us -> 106 us (level)
    pallas_call x1, Pallas kernels: 14.2 us -> 10.7 us  [body(): pl.pallas_call(finish_kernel, out_shape=(shape((len(LINKS), SLOTS - SPLIT...]
    pallas_call x1, Pallas kernels: 83.9 us -> 87.4 us  [body(): pl.pallas_call(gather_kernel, out_shape=(shape((n_rows, QUARTERS, unit, d...]
where the time goes in v10:
time: 106 us
  Pallas kernels  105 us (99%)
    pallas_call x1, Pallas kernels, body(): pl.pallas_call(gather_kernel, out_shape=(shape((n_rows, QUARTERS, unit, d...  87.4 us
    pallas_call x1, Pallas kernels, body(): pl.pallas_call(finish_kernel, out_shape=(shape((len(LINKS), SLOTS - SPLIT...  10.7 us
    pallas_call x1, Pallas kernels, body(): pl.pallas_call(write_kernel, out_shape=(*outs, shape((8, 128), f32)), in_...  5.7 us

profile of v10, /device:TPU:1, one launch (start us, length us, event | category | flops | bytes accessed | tf_op | source)
XLA Modules:
  0.0 105.9 jit_solution(4422291162695271801)
XLA Ops:
  0.6 87.4 %gather.1 = (bf16[16,4,288,512]{3,2,1,0:T(8,128)(2,1)S(1)}, bf16[64,128]{1,0:T(8,128)(2,1)S(1)}) custom-call(bf16[512,1024]{1,0:T(8,128)(2,1)} %train_query.1, bf16[64,512]{1,0:T(8,128)(2,1)} %bitcast.8, bf16[64,1024]{1,0:T(8,128)(2,1)} %high_query.1, bf16[64,512]{1,0:T(8,128)(2,1)} %bitcast.9, bf16[64,512]{1,0:T(8,128)(2,1)} %bitcast.10, ...), custom_call_target="tpu_custom_call" | custom-call | tf_op jit(solution)/shard_map/gather/pallas_call | solution.py:466
  88.0 5.7 %write.1 = (bf16[1024,8192]{1,0:T(8,128)(2,1)}, bf16[64,8192]{1,0:T(8,128)(2,1)}, bf16[64,8192]{1,0:T(8,128)(2,1)}, f32[8,128]{1,0:T(8,128)S(1)}) custom-call(bf16[16,4,288,512]{3,2,1,0:T(8,128)(2,1)S(1)} %get-tuple-element.14.whole), custom_call_target="tpu_custom_call" | custom-call | tf_op jit(solution)/shard_map/write/pallas_call | solution.py:512
  93.7 10.7 %finish.1.rest = bf16[4,2,288,512]{3,2,1,0:T(8,128)(2,1)S(1)} custom-call(bf16[16,4,288,512]{3,2,1,0:T(8,128)(2,1)S(1)} %get-tuple-element.14.whole, f32[8,128]{1,0:T(8,128)S(1)} %get-tuple-element.15.token), custom_call_target="tpu_custom_call" | custom-call | tf_op jit(solution)/shard_map/finish/pallas_call | solution.py:521
  104.4 1.4 %write_rest.1 = (bf16[1024,8192]{1,0:T(8,128)(2,1)}, bf16[64,8192]{1,0:T(8,128)(2,1)}, bf16[64,8192]{1,0:T(8,128)(2,1)}, bf16[64,128]{1,0:T(8,128)(2,1)}) custom-call(bf16[16,4,288,512]{3,2,1,0:T(8,128)(2,1)S(1)} %get-tuple-element.14.whole, bf16[4,2,288,512]{3,2,1,0:T(8,128)(2,1)S(1)} %finish.1.rest, ...), custom_call_target="tpu_custom_call", output_to_operand_aliasing={{0}: (3, {}), {1}: (4, {}), {2}: (5, {})} | custom-call | tf_op jit(solution)/shard_map/write_rest/pallas_call | solution.py:532

commit v11 on v10

--- a/solution.py
+++ b/solution.py
@@ -13,7 +13,7 @@
 LINKS = ((0, 1), (0, -1), (1, 0), (-1, 0))
 LATE = 1
 SPLIT = 13
-HEAD_START = 2900
+HEAD_START = 3800
 LEAD = 2
 ORDER = (0, 2, 1, 3)
 

time: 106 us -> 107 us (level)
    pallas_call x1, Pallas kernels: 10.7 us -> 12.5 us  [body(): pl.pallas_call(finish_kernel, out_shape=(shape((len(LINKS), SLOTS - SPLIT...]
where the time goes in v11:
time: 107 us
  Pallas kernels  106 us (99%)
    pallas_call x1, Pallas kernels, body(): pl.pallas_call(gather_kernel, out_shape=(shape((n_rows, QUARTERS, unit, d...  86.5 us
    pallas_call x1, Pallas kernels, body(): pl.pallas_call(finish_kernel, out_shape=(shape((len(LINKS), SLOTS - SPLIT...  12.5 us
    pallas_call x1, Pallas kernels, body(): pl.pallas_call(write_kernel, out_shape=(*outs, shape((8, 128), f32)), in_...  5.7 us

profile of v11, /device:TPU:1, one launch (start us, length us, event | category | flops | bytes accessed | tf_op | source)
XLA Modules:
  0.0 106.8 jit_solution(9543159542965527102)
XLA Ops:
  0.6 86.5 %gather.1 = (bf16[16,4,288,512]{3,2,1,0:T(8,128)(2,1)S(1)}, bf16[64,128]{1,0:T(8,128)(2,1)S(1)}) custom-call(bf16[512,1024]{1,0:T(8,128)(2,1)} %train_query.1, bf16[64,512]{1,0:T(8,128)(2,1)} %bitcast.8, bf16[64,1024]{1,0:T(8,128)(2,1)} %high_query.1, bf16[64,512]{1,0:T(8,128)(2,1)} %bitcast.9, bf16[64,512]{1,0:T(8,128)(2,1)} %bitcast.10, ...), custom_call_target="tpu_custom_call" | custom-call | tf_op jit(solution)/shard_map/gather/pallas_call | solution.py:466
  87.1 5.7 %write.1 = (bf16[1024,8192]{1,0:T(8,128)(2,1)}, bf16[64,8192]{1,0:T(8,128)(2,1)}, bf16[64,8192]{1,0:T(8,128)(2,1)}, f32[8,128]{1,0:T(8,128)S(1)}) custom-call(bf16[16,4,288,512]{3,2,1,0:T(8,128)(2,1)S(1)} %get-tuple-element.14.whole), custom_call_target="tpu_custom_call" | custom-call | tf_op jit(solution)/shard_map/write/pallas_call | solution.py:512
  92.8 12.5 %finish.1.rest = bf16[4,2,288,512]{3,2,1,0:T(8,128)(2,1)S(1)} custom-call(bf16[16,4,288,512]{3,2,1,0:T(8,128)(2,1)S(1)} %get-tuple-element.14.whole, f32[8,128]{1,0:T(8,128)S(1)} %get-tuple-element.15.token), custom_call_target="tpu_custom_call" | custom-call | tf_op jit(solution)/shard_map/finish/pallas_call | solution.py:521
  105.3 1.4 %write_rest.1 = (bf16[1024,8192]{1,0:T(8,128)(2,1)}, bf16[64,8192]{1,0:T(8,128)(2,1)}, bf16[64,8192]{1,0:T(8,128)(2,1)}, bf16[64,128]{1,0:T(8,128)(2,1)}) custom-call(bf16[16,4,288,512]{3,2,1,0:T(8,128)(2,1)S(1)} %get-tuple-element.14.whole, bf16[4,2,288,512]{3,2,1,0:T(8,128)(2,1)S(1)} %finish.1.rest, ...), custom_call_target="tpu_custom_call", output_to_operand_aliasing={{0}: (3, {}), {1}: (4, {}), {2}: (5, {})} | custom-call | tf_op jit(solution)/shard_map/write_rest/pallas_call | solution.py:532

commit v12 on v8

--- a/solution.py
+++ b/solution.py
@@ -112,7 +112,7 @@
     norm_train, norm_step,
     whole, norm,
     tq, lq, hq, tk, lk, hk, tv, lv, hv, nt, ns, fresh, ring, lines, ordered,
-    load_sem, send_sem, recv_sem, fresh_sem, column_sem, line_sem, norm_sem,
+    load_sem, send_sem, recv_sem, small_send, small_recv, norm_send,
 ):
     me = Place()
     wide = tq.shape[1]
@@ -139,31 +139,46 @@
         def _():
             signal_all(barrier, [me.neighbour((0, 2))] + [me.plane(n) for n in range(1, n_planes)])
 
-    loads = {}
-
-    def load(name, src, dst):
-        copy = pltpu.make_async_copy(src, dst, load_sem.at[len(loads)])
-        copy.start()
-        loads[name] = copy
-
+    part_of_high = part // 2
+    rest_of_high = wide - part_of_high
     pieces = [(ORDER[0], 0, part // 2), (ORDER[0], part // 2, part)] + [(q, 0, part) for q in ORDER[1:]]
-    load("lq", low_query, lq)
-    load("hq", high_query, hq)
-    for n, (q, start, end) in enumerate(pieces):
+
+    def piece_load(n):
+        q, start, end = pieces[n]
         cols = pl.ds(q * part + start, end - start)
-        load(n, train_query.at[:, cols], tq.at[:, cols])
-        if n == 0:
-            greet()
-            load("nt", norm_train, nt)
-            load("ns", norm_step, ns)
-        if n == 1:
-            load("tk", train_key, tk)
-            load("lk", low_key, lk)
-            load("hk", high_key, hk)
-        if n == 2:
-            load("tv", train_value, tv)
-            load("lv", low_value, lv)
-            load("hv", high_value, hv)
+        return train_query.at[:, cols], tq.at[:, cols]
+
+    first, rest = pl.ds(0, part_of_high), pl.ds(part_of_high, rest_of_high)
+    together = [
+        [(low_query, lq), (high_query.at[:, first], hq.at[:, first]), piece_load(0)],
+        [(high_query.at[:, rest], hq.at[:, rest]), piece_load(1), (train_key, tk), (low_key, lk)],
+        [piece_load(2), (train_value, tv), (low_value, lv)],
+        [piece_load(3)],
+        [piece_load(4)],
+        [(high_key, hk)],
+        [(high_value, hv)],
+        [(norm_train, nt)],
+        [(norm_step, ns)],
+    ]
+
+    def start_loads(group):
+        for src, dst in together[group]:
+            pltpu.make_async_copy(src, dst, load_sem.at[group]).start()
+
+    def wait_loads(group):
+        if len(together[group]) == 1:
+            src, dst = together[group][0]
+        else:
+            size = sum(dst.shape[0] * dst.shape[1] for _, dst in together[group])
+            rows = pl.ds(0, size // wide)
+            assert size % (8 * wide) == 0
+            src, dst = train_query.at[rows], tq.at[rows]
+        pltpu.make_async_copy(src, dst, load_sem.at[group]).wait()
+
+    start_loads(0)
+    greet()
+    for group in (7, 8, 1, 5, 2, 6, 3, 4):
+        start_loads(group)
 
     def merged(train, high, low):
         return train.astype(jnp.float32) + lax.dot_general(
@@ -189,26 +204,26 @@
         return pl.when(me.core == LATE if core == LATE else me.core != LATE)
 
     def fresh_copy():
-        return remote(fresh, ring.at[me.y * SIDE + me.z], fresh_sem.at[0], fresh_sem.at[1], (me.y, me.col))
+        return remote(fresh, ring.at[me.y * SIDE + me.z], small_send, small_recv.at[0], (me.y, me.col))
 
     def column_copy():
         part_of_ring = ring.at[pl.ds(me.y * SIDE, SIDE)]
-        return remote(part_of_ring, part_of_ring, column_sem.at[0], column_sem.at[1], (LEAD, me.col))
+        return remote(part_of_ring, part_of_ring, small_send, small_recv.at[1], (LEAD, me.col))
 
     def ring_lines(count, sem):
         some = ring.at[pl.ds(0, count)]
-        return remote(some, some, sem.at[0], sem.at[1], me.partner())
+        return remote(some, some, small_send, sem, me.partner())
 
     def norm_copy(off):
-        return remote(norm, norm, norm_sem.at[0], norm_sem.at[1], me.neighbour(off))
+        return remote(norm, norm, norm_send, small_recv.at[3], me.neighbour(off))
 
     def norm_sent(count):
         some = whole.at[0, 0, pl.ds(0, count * norm.shape[0] * norm.shape[1] // whole.shape[3])]
-        remote(some, some, norm_sem.at[0], norm_sem.at[1], me.partner()).wait_send()
+        remote(some, some, norm_send, small_recv.at[3], me.partner()).wait_send()
 
     def make_fresh():
-        loads["nt"].wait()
-        loads["ns"].wait()
+        wait_loads(7)
+        wait_loads(8)
         values = nt[...] + ns[...]
         fresh[...] = jnp.concatenate([values, values], axis=1)
 
@@ -221,11 +236,9 @@
         def _():
             fresh_copy().start()
 
-    loads["lq"].wait()
-    loads["hq"].wait()
     for n, (q, start, end) in enumerate(pieces):
         cols = pl.ds(q * part + start, end - start)
-        loads[n].wait()
+        wait_loads(n)
         if n == 1:
             make_fresh()
         whole[me.row, q, start:end, :] = merged(tq[:, cols].T, hq[:, cols], lq[...]).astype(whole.dtype)
@@ -247,11 +260,9 @@
 
         if end == part:
             if n == 1:
-                for name in ("tk", "lk", "hk"):
-                    loads[name].wait()
+                wait_loads(5)
             if n == 2:
-                for name in ("tv", "lv", "hv"):
-                    loads[name].wait()
+                wait_loads(6)
             train, low, high = (tk, lk, hk) if q < 2 else (tv, lv, hv)
             small = merged(train[...], high[...], low[...]).astype(whole.dtype)
             half = small.shape[0] // 2
@@ -271,7 +282,7 @@
 
             @pl.when(top)
             def _():
-                ring_lines(len(column), fresh_sem).wait_recv()
+                ring_lines(len(column), small_recv.at[0]).wait_recv()
 
             @pl.when(head)
             def _():
@@ -281,13 +292,13 @@
 
             @pl.when(leader)
             def _():
-                ring_lines(len(heads) * SIDE, column_sem).wait_recv()
+                ring_lines(len(heads) * SIDE, small_recv.at[1]).wait_recv()
                 in_order = [ring[(i % SIDE) * SIDE + i // SIDE] for i in range(blocks)]
                 lines[me.col] = jnp.concatenate(in_order, axis=0)
                 for n in range(1, n_planes):
-                    remote(lines.at[me.col], lines.at[me.col], line_sem.at[0], line_sem.at[1], me.plane(n)).start()
+                    remote(lines.at[me.col], lines.at[me.col], small_send, small_recv.at[2], me.plane(n)).start()
                 some = lines.at[pl.ds(0, n_planes - 1)]
-                remote(some, some, line_sem.at[0], line_sem.at[1], me.partner()).wait()
+                remote(some, some, small_send, small_recv.at[2], me.partner()).wait()
                 lane = lax.broadcasted_iota(jnp.int32, lines.shape[1:], 1)
                 for x in range(SIDE):
                     both = jnp.where(lane < lines.shape[2] // CORES, lines[CORES * x], lines[CORES * x + 1])
@@ -478,13 +489,12 @@
             pltpu.VMEM((n_rows, 1, line), f32),
             pltpu.VMEM((n_cols, n_rows, line), f32),
             pltpu.VMEM((SIDE * n_rows, line), f32),
-            dma((15,)),
+            dma((9,)),
             dma(()),
             dma((len(GROUPS),)),
-            dma((2,)),
-            dma((2,)),
-            dma((2,)),
-            dma((2,)),
+            dma(()),
+            dma((4,)),
+            dma(()),
         ],
         compiler_params=pltpu.CompilerParams(
             collective_id=0, has_side_effects=True, vmem_limit_bytes=24 * 2**20

time: 106 us -> 106 us (level)
  no operation moved by 1% of the time
where the time goes in v12:
time: 106 us
  Pallas kernels  105 us (99%)
    pallas_call x1, Pallas kernels, body(): pl.pallas_call(gather_kernel, out_shape=(shape((n_rows, QUARTERS, unit, d...  83.9 us
    pallas_call x1, Pallas kernels, body(): pl.pallas_call(finish_kernel, out_shape=(shape((len(LINKS), SLOTS - SPLIT...  14.2 us
    pallas_call x1, Pallas kernels, body(): pl.pallas_call(write_kernel, out_shape=(*outs, shape((8, 128), f32)), in_...  5.35 us

profile of v12, /device:TPU:1, one launch (start us, length us, event | category | flops | bytes accessed | tf_op | source)
XLA Modules:
  0.0 106.0 jit_solution(12357738464342837106)
XLA Ops:
  0.6 83.9 %gather.1 = (bf16[16,4,288,512]{3,2,1,0:T(8,128)(2,1)S(1)}, bf16[64,128]{1,0:T(8,128)(2,1)S(1)}) custom-call(bf16[512,1024]{1,0:T(8,128)(2,1)} %train_query.1, bf16[64,512]{1,0:T(8,128)(2,1)} %bitcast.8, bf16[64,1024]{1,0:T(8,128)(2,1)} %high_query.1, bf16[64,512]{1,0:T(8,128)(2,1)} %bitcast.9, bf16[64,512]{1,0:T(8,128)(2,1)} %bitcast.10, ...), custom_call_target="tpu_custom_call" | custom-call | tf_op jit(solution)/shard_map/gather/pallas_call | solution.py:468
  84.5 5.3 %write.1 = (bf16[1024,8192]{1,0:T(8,128)(2,1)}, bf16[64,8192]{1,0:T(8,128)(2,1)}, bf16[64,8192]{1,0:T(8,128)(2,1)}, f32[8,128]{1,0:T(8,128)S(1)}) custom-call(bf16[16,4,288,512]{3,2,1,0:T(8,128)(2,1)S(1)} %get-tuple-element.14.whole), custom_call_target="tpu_custom_call" | custom-call | tf_op jit(solution)/shard_map/write/pallas_call | solution.py:513
  89.9 14.2 %finish.1.rest = bf16[4,3,288,512]{3,2,1,0:T(8,128)(2,1)S(1)} custom-call(bf16[16,4,288,512]{3,2,1,0:T(8,128)(2,1)S(1)} %get-tuple-element.14.whole, f32[8,128]{1,0:T(8,128)S(1)} %get-tuple-element.15.token), custom_call_target="tpu_custom_call" | custom-call | tf_op jit(solution)/shard_map/finish/pallas_call | solution.py:522
  104.1 1.8 %write_rest.1 = (bf16[1024,8192]{1,0:T(8,128)(2,1)}, bf16[64,8192]{1,0:T(8,128)(2,1)}, bf16[64,8192]{1,0:T(8,128)(2,1)}, bf16[64,128]{1,0:T(8,128)(2,1)}) custom-call(bf16[16,4,288,512]{3,2,1,0:T(8,128)(2,1)S(1)} %get-tuple-element.14.whole, bf16[4,3,288,512]{3,2,1,0:T(8,128)(2,1)S(1)} %finish.1.rest, ...), custom_call_target="tpu_custom_call", output_to_operand_aliasing={{0}: (3, {}), {1}: (4, {}), {2}: (5, {})} | custom-call | tf_op jit(solution)/shard_map/write_rest/pallas_call | solution.py:533

commit v13 on v12

--- a/solution.py
+++ b/solution.py
@@ -11,7 +11,7 @@
 QUARTERS = 4
 CORES = 2
 LINKS = ((0, 1), (0, -1), (1, 0), (-1, 0))
-LATE = 1
+LATE = 0
 SPLIT = 12
 LEAD = 2
 ORDER = (0, 2, 1, 3)

time: 106 us -> 107 us (level)
  the two profiles are of different devices: /device:TPU:1 before, /device:TPU:0 now
where the time goes in v13:
time: 107 us
  Pallas kernels  107 us (100%)
    pallas_call x1, Pallas kernels, body(): pl.pallas_call(gather_kernel, out_shape=(shape((n_rows, QUARTERS, unit, d...  85.2 us
    pallas_call x1, Pallas kernels, body(): pl.pallas_call(finish_kernel, out_shape=(shape((len(LINKS), SLOTS - SPLIT...  14.3 us
    pallas_call x1, Pallas kernels, body(): pl.pallas_call(write_kernel, out_shape=(*outs, shape((8, 128), f32)), in_...  5.35 us

profile of v13, /device:TPU:0, one launch (start us, length us, event | category | flops | bytes accessed | tf_op | source)
XLA Modules:
  0.0 107.3 jit_solution(15617899889220783731)
XLA Ops:
  0.6 85.2 %gather.1 = (bf16[16,4,288,512]{3,2,1,0:T(8,128)(2,1)S(1)}, bf16[64,128]{1,0:T(8,128)(2,1)S(1)}) custom-call(bf16[512,1024]{1,0:T(8,128)(2,1)} %train_query.1, bf16[64,512]{1,0:T(8,128)(2,1)} %bitcast.8, bf16[64,1024]{1,0:T(8,128)(2,1)} %high_query.1, bf16[64,512]{1,0:T(8,128)(2,1)} %bitcast.9, bf16[64,512]{1,0:T(8,128)(2,1)} %bitcast.10, ...), custom_call_target="tpu_custom_call" | custom-call | tf_op jit(solution)/shard_map/gather/pallas_call | solution.py:468
  85.8 5.3 %write.1 = (bf16[1024,8192]{1,0:T(8,128)(2,1)}, bf16[64,8192]{1,0:T(8,128)(2,1)}, bf16[64,8192]{1,0:T(8,128)(2,1)}, f32[8,128]{1,0:T(8,128)S(1)}) custom-call(bf16[16,4,288,512]{3,2,1,0:T(8,128)(2,1)S(1)} %get-tuple-element.14.whole), custom_call_target="tpu_custom_call" | custom-call | tf_op jit(solution)/shard_map/write/pallas_call | solution.py:513
  91.2 14.3 %finish.1.rest = bf16[4,3,288,512]{3,2,1,0:T(8,128)(2,1)S(1)} custom-call(bf16[16,4,288,512]{3,2,1,0:T(8,128)(2,1)S(1)} %get-tuple-element.14.whole, f32[8,128]{1,0:T(8,128)S(1)} %get-tuple-element.15.token), custom_call_target="tpu_custom_call" | custom-call | tf_op jit(solution)/shard_map/finish/pallas_call | solution.py:522
  105.5 1.8 %write_rest.1 = (bf16[1024,8192]{1,0:T(8,128)(2,1)}, bf16[64,8192]{1,0:T(8,128)(2,1)}, bf16[64,8192]{1,0:T(8,128)(2,1)}, bf16[64,128]{1,0:T(8,128)(2,1)}) custom-call(bf16[16,4,288,512]{3,2,1,0:T(8,128)(2,1)S(1)} %get-tuple-element.14.whole, bf16[4,3,288,512]{3,2,1,0:T(8,128)(2,1)S(1)} %finish.1.rest, ...), custom_call_target="tpu_custom_call", output_to_operand_aliasing={{0}: (3, {}), {1}: (4, {}), {2}: (5, {})} | custom-call | tf_op jit(solution)/shard_map/write_rest/pallas_call | solution.py:533

commit v14 on v12

--- a/solution.py
+++ b/solution.py
@@ -373,15 +373,18 @@
         remote(rest, rest, send_sem, recv_sem, me.partner()).wait()
 
 
-def write_unit(source, block, quarter, outs, sems):
+def write_unit(source, block, quarter, outs, sems, large=None):
     out_query, out_key, out_value = outs
     rows, depth = source.shape
     part = out_query.shape[0] // QUARTERS
     half = rows - part
     at = pl.ds(pl.multiple_of(block * depth, depth), depth)
     small = (out_key if quarter < 2 else out_value).at[pl.ds((quarter % 2) * half, half), at]
-    pltpu.make_async_copy(source.at[pl.ds(0, part)], out_query.at[pl.ds(quarter * part, part), at], sems[0]).start()
-    pltpu.make_async_copy(source.at[pl.ds(part, half)], small, sems[1 + quarter // 2]).start()
+    if large is not False:
+        query = out_query.at[pl.ds(quarter * part, part), at]
+        pltpu.make_async_copy(source.at[pl.ds(0, part)], query, sems[0]).start()
+    if large is not True:
+        pltpu.make_async_copy(source.at[pl.ds(part, half)], small, sems[1 + quarter // 2]).start()
 
 
 def wait_units(count, unit_bytes, out, sem):
@@ -424,9 +427,10 @@
     @pl.when(me.core == LATE)
     def _():
         first = sem.at[0]
-        for link, slot in LAST:
-            off, q = arriving(link, slot)
-            write_unit(rest.at[link, slot - SPLIT], me.at(off), q, outs, (first, first, first))
+        for large in (True, False):
+            for link, slot in LAST:
+                off, q = arriving(link, slot)
+                write_unit(rest.at[link, slot - SPLIT], me.at(off), q, outs, (first, first, first), large)
         wait_units(len(LAST), unit_bytes_of(whole), out_query, first)
 
     @pl.when(me.core != LATE)

time: 106 us -> 106 us (level)
  no operation moved by 1% of the time
where the time goes in v14:
time: 106 us
  Pallas kernels  105 us (99%)
    pallas_call x1, Pallas kernels, body(): pl.pallas_call(gather_kernel, out_shape=(shape((n_rows, QUARTERS, unit, d...  83.9 us
    pallas_call x1, Pallas kernels, body(): pl.pallas_call(finish_kernel, out_shape=(shape((len(LINKS), SLOTS - SPLIT...  14.2 us
    pallas_call x1, Pallas kernels, body(): pl.pallas_call(write_kernel, out_shape=(*outs, shape((8, 128), f32)), in_...  5.35 us

profile of v14, /device:TPU:1, one launch (start us, length us, event | category | flops | bytes accessed | tf_op | source)
XLA Modules:
  0.0 106.0 jit_solution(18265506236459136245)
XLA Ops:
  0.6 83.9 %gather.1 = (bf16[16,4,288,512]{3,2,1,0:T(8,128)(2,1)S(1)}, bf16[64,128]{1,0:T(8,128)(2,1)S(1)}) custom-call(bf16[512,1024]{1,0:T(8,128)(2,1)} %train_query.1, bf16[64,512]{1,0:T(8,128)(2,1)} %bitcast.8, bf16[64,1024]{1,0:T(8,128)(2,1)} %high_query.1, bf16[64,512]{1,0:T(8,128)(2,1)} %bitcast.9, bf16[64,512]{1,0:T(8,128)(2,1)} %bitcast.10, ...), custom_call_target="tpu_custom_call" | custom-call | tf_op jit(solution)/shard_map/gather/pallas_call | solution.py:472
  84.5 5.3 %write.1 = (bf16[1024,8192]{1,0:T(8,128)(2,1)}, bf16[64,8192]{1,0:T(8,128)(2,1)}, bf16[64,8192]{1,0:T(8,128)(2,1)}, f32[8,128]{1,0:T(8,128)S(1)}) custom-call(bf16[16,4,288,512]{3,2,1,0:T(8,128)(2,1)S(1)} %get-tuple-element.14.whole), custom_call_target="tpu_custom_call" | custom-call | tf_op jit(solution)/shard_map/write/pallas_call | solution.py:517
  89.9 14.2 %finish.1.rest = bf16[4,3,288,512]{3,2,1,0:T(8,128)(2,1)S(1)} custom-call(bf16[16,4,288,512]{3,2,1,0:T(8,128)(2,1)S(1)} %get-tuple-element.14.whole, f32[8,128]{1,0:T(8,128)S(1)} %get-tuple-element.15.token), custom_call_target="tpu_custom_call" | custom-call | tf_op jit(solution)/shard_map/finish/pallas_call | solution.py:526
  104.1 1.8 %write_rest.1 = (bf16[1024,8192]{1,0:T(8,128)(2,1)}, bf16[64,8192]{1,0:T(8,128)(2,1)}, bf16[64,8192]{1,0:T(8,128)(2,1)}, bf16[64,128]{1,0:T(8,128)(2,1)}) custom-call(bf16[16,4,288,512]{3,2,1,0:T(8,128)(2,1)S(1)} %get-tuple-element.14.whole, bf16[4,3,288,512]{3,2,1,0:T(8,128)(2,1)S(1)} %finish.1.rest, ...), custom_call_target="tpu_custom_call", output_to_operand_aliasing={{0}: (3, {}), {1}: (4, {}), {2}: (5, {})} | custom-call | tf_op jit(solution)/shard_map/write_rest/pallas_call | solution.py:537
